TPU v7x, 128 devices: a whole 4x4x4 slice. The times are simulated.
128 devices in a mesh: gx: 8 (over z, y_lo), gy: 8 (over x, core), gz: 2 (over y_hi).
Axes of the slice: x: 4, y: 4 (y_hi: 2, y_lo: 2; y = y_hi * 2 + y_lo), z: 4, core: 2. Of those that a mesh axis runs over, the one named last changes fastest.
Arguments:
- right_side: float32 [512, 512, 512], P('gx', 'gy', 'gz'), may hold values from -6 to 6
- guess: float32 [512, 512, 512], P('gx', 'gy', 'gz'), may hold values from -4 to 4
Outputs:
- updated: float32 [512, 512, 512], P('gx', 'gy', 'gz')
- new_residual: float32 [512, 512, 512], P('gx', 'gy', 'gz')
- res_norm: float32 [], replicated
All inputs are finite; a program needn't handle non-finite values.
Results may differ from a plain program's by a relative error of at most 0.0003.
Values sent between devices are 32-bit elements; how exact they have to be, the bound alone decides.
A program may use at most 128 MiB of HBM per device.

v0:
```python
import functools
import math

import jax
import jax.numpy as jnp
from jax import lax
from jax.sharding import Mesh
from jax.sharding import PartitionSpec as P

COARSEN = 4
GX_GY_GZ = ("gx_0", "gx_1", "gy_0", "gy_1", "gz")
GX = ("gx_0", "gx_1")
GY = ("gy_0", "gy_1")
GX_GZ = ("gx_0", "gx_1", "gz")


screen = 0.002
exact_prec = lax.Precision.HIGHEST


def with_halo(shard, sides, width):
    edges = {}
    for axis, dim in sides:
        devices, length = (lax.axis_size(axis), shard.shape[dim])
        up = [(i, (i + 1) % devices) for i in range(devices)]
        last = lax.slice_in_dim(shard, length - width, length, axis=dim)
        leading = lax.slice_in_dim(shard, 0, width, axis=dim)
        edges[dim] = (
            lax.ppermute(last, axis, up),
            lax.ppermute(leading, axis, [(b, a) for a, b in up]),
        )
    done = []
    for _, dim in sides:
        low, high = edges[dim]
        around = [(width, width) if d in done else (0, 0) for d in range(shard.ndim)]
        shard = jnp.concatenate([jnp.pad(low, around), shard, jnp.pad(high, around)], axis=dim)
        done.append(dim)
    return shard


def over_axes(shard, axes):
    return functools.reduce(lax.psum, axes, shard)


def neighbours(padded):
    total = padded[2:, 1:-1, 1:-1] + padded[:-2, 1:-1, 1:-1]
    total = total + padded[1:-1, 2:, 1:-1] + padded[1:-1, :-2, 1:-1]
    total = total + padded[1:-1, 1:-1, 2:] + padded[1:-1, 1:-1, :-2]
    return total


def hartley(length):
    index = jnp.arange(length, dtype=jnp.int32)
    product = index[:, None] * index[None, :] % length
    angle = 2.0 * math.pi * product.astype(jnp.float32) / length
    return jnp.cos(angle) + jnp.sin(angle)


def eigen_line(index, length):
    phase = (index % length).astype(jnp.float32)
    return (2.0 - 2.0 * jnp.cos(2.0 * math.pi * phase / length)) / (COARSEN * COARSEN)


def along_first(values, matrix):
    return jnp.einsum("jab,jk->kab", values, matrix, precision=exact_prec)


def along_second(values, matrix):
    return jnp.einsum("ajb,jk->akb", values, matrix, precision=exact_prec)


def along_third(values, matrix):
    return jnp.einsum("abj,jk->abk", values, matrix, precision=exact_prec)


def fold_table(fine, coarse_len):
    fine_index = jnp.arange(fine, dtype=jnp.int32) // COARSEN
    coarse_index = jnp.arange(coarse_len, dtype=jnp.int32)
    return (fine_index[:, None] == coarse_index[None, :]).astype(jnp.float32)


def per_device(right_side, guess):
    diag_value = 6.0 + screen
    padded = with_halo(guess, ((GX, 0), (GY, 1), ("gz", 2)), 1)
    residual_now = right_side - (diag_value * guess - neighbours(padded))
    first_sweep = residual_now / diag_value
    padded_sweep = with_halo(first_sweep, ((GX, 0), (GY, 1), ("gz", 2)), 1)
    local_fix = (residual_now + neighbours(padded_sweep)) / diag_value
    block_x, block_y, block_z = guess.shape
    coarse_x = block_x // COARSEN
    coarse_y = block_y // COARSEN
    coarse_z = block_z // COARSEN
    fold_z = fold_table(block_z, coarse_z)
    planes = residual_now.reshape(coarse_x, COARSEN, coarse_y, COARSEN, block_z).sum(axis=(1, 3))
    coarse = along_third(planes, fold_z) / (COARSEN * COARSEN * COARSEN)
    length_x = coarse_x * lax.axis_size(GX)
    length_y = coarse_y * lax.axis_size(GY)
    length_z = coarse_z * lax.axis_size("gz")
    scale = 1.0 / (length_x * length_y * length_z)
    table_x = hartley(length_x)
    table_y = hartley(length_y)
    table_z = hartley(length_z)
    spectra = lax.all_to_all(coarse, "gz", split_axis=0, concat_axis=2, tiled=True)
    spectra = along_third(spectra, table_z)
    spectra = lax.all_to_all(spectra, GY, split_axis=2, concat_axis=1, tiled=True)
    spectra = along_second(spectra, table_y)
    spectra = lax.all_to_all(spectra, GX_GZ, split_axis=1, concat_axis=0, tiled=True)
    spectra = along_first(spectra, table_x)
    width_y = spectra.shape[1]
    width_z = spectra.shape[2]
    index_x = jnp.arange(length_x, dtype=jnp.int32)
    index_y = (
        lax.axis_index(GX) * lax.axis_size("gz") + lax.axis_index("gz")
    ) * width_y + jnp.arange(width_y, dtype=jnp.int32)
    index_z = lax.axis_index(GY) * width_z + jnp.arange(width_z, dtype=jnp.int32)
    eigen_sum = (
        screen
        + eigen_line(index_x, length_x)[:, None, None]
        + eigen_line(index_y, length_y)[None, :, None]
        + eigen_line(index_z, length_z)[None, None, :]
    )
    spectra = along_first(spectra / eigen_sum, table_x) * scale
    spectra = lax.all_to_all(spectra, GX_GZ, split_axis=0, concat_axis=1, tiled=True)
    spectra = along_second(spectra, table_y)
    spectra = lax.all_to_all(spectra, GY, split_axis=1, concat_axis=2, tiled=True)
    spectra = along_third(spectra, table_z)
    correction = lax.all_to_all(spectra, "gz", split_axis=2, concat_axis=0, tiled=True)
    spread = jnp.einsum("abk,jk->abj", correction, fold_z, precision=exact_prec)
    prolonged = jnp.broadcast_to(
        spread[:, None, :, None, :], (coarse_x, COARSEN, coarse_y, COARSEN, block_z)
    ).reshape(block_x, block_y, block_z)
    updated = guess + local_fix + prolonged
    padded_new = with_halo(updated, ((GX, 0), (GY, 1), ("gz", 2)), 1)
    new_residual = right_side - (diag_value * updated - neighbours(padded_new))
    total = over_axes(jnp.sum(new_residual * new_residual), GX_GY_GZ)
    return (updated, new_residual, jnp.sqrt(total))


def solution(mesh):
    finer = Mesh(
        mesh.devices.reshape(4, 2, 4, 2, mesh.shape["gz"]), ("gx_0", "gx_1", "gy_0", "gy_1", "gz")
    )
    in_specs = (P(GX, GY, "gz"), P(GX, GY, "gz"))
    out_specs = (P(GX, GY, "gz"), P(GX, GY, "gz"), P())
    return jax.shard_map(
        per_device, mesh=finer, in_specs=in_specs, out_specs=out_specs, check_vma=False
    )
```

profile of v0, /device:TPU:1, one launch (start us, length us, event | category | flops | bytes accessed | tf_op | source)
XLA Modules:
  0.0 258.1 jit_solution(824009369090774762)
XLA Ops:
  0.6 0.9 fusion.104
  1.5 2.2 collective-permute-start.1
  3.7 3.6 %collective-permute-start = (f32[1,64,256]{2,1,0:T(8,128)S(1)}, f32[1,64,256]{2,1,0:T(8,128)S(1)}, u32[]{:S(2)}, u32[]{:S(2)}) collective-permute-start(f32[1,64,256]{2,1,0:T(8,128)S(1)} %get-tuple-element.26), channel_id=1, source_target_pairs={{16,0},{32,16},{48,32},{64,48},{80,64},{96,80},{112,96},{0,112},{1... | collective-permute-start | bytes 196616 | tf_op jit(solution)/shard_map/ppermute | solution.py:30
  7.3 4.4 %fusion.102 = (f32[64,64,1]{2,1,0:T(8,128)}, f32[64,64,1]{2,1,0:T(8,128)S(1)}) fusion(f32[64,64,256]{2,1,0:T(8,128)} %param.3), kind=kLoop, calls=%fused_computation.174 | loop fusion | bytes 65536 | tf_op jit(solution)/shard_map/slice | solution.py:27
  11.6 2.3 copy.76
  13.9 2.7 %collective-permute-start.4 = (f32[64,64,1]{1,0,2:T(8,128)S(1)}, f32[64,64,1]{1,0,2:T(8,128)S(1)}, u32[]{:S(2)}, u32[]{:S(2)}) collective-permute-start(f32[64,64,1]{1,0,2:T(8,128)S(1)} %copy.76), channel_id=1, source_target_pairs={{1,0},{0,1},{3,2},{2,3},{5,4},{4,5},{7,6},{6,7},{9,8},{8,9},{11,10... | collective-permute-start | bytes 49160 | tf_op jit(solution)/shard_map/ppermute | solution.py:30
  16.6 1.3 copy.77
  18.2 1.9 fusion.103
  20.2 1.5 collective-permute-start.2
  22.9 1.1 collective-permute-start.3
  24.0 0.7 copy.50
  24.7 2.0 copy.52
  27.3 4.8 %constant_dynamic-update-slice_fusion.1 = f32[66,64,256]{2,1,0:T(8,128)} fusion(f32[66,64,256]{2,1,0:T(8,128)} %constant_dynamic-update-slice_fusion.2, f32[64,64,256]{2,1,0:T(8,128)} %param.3), kind=kLoop, calls=%fused_computation.109 | loop fusion | bytes 8388608
  32.9 18.6 %broadcast_multiply_fusion = (f32[64,64,256]{2,1,0:T(8,128)}, f32[64,64,256]{2,1,0:T(8,128)}) fusion(f32[64,64,256]{2,1,0:T(8,128)} %param.2, f32[66,1,256]{2,1,0:T(1,128)S(1)} %pad.38, f32[66,64,256]{2,1,0:T(8,128)} %constant_dynamic-update-slice_fusion, f32[66,1,256]{2,1,0:T(1,128)S(1)} %pad.39, f32[64,64,1]{2,1,0:T(8,128)} %copy.52, ...), kind=kLoop, calls=%fused_computation.78 | loop fusion | flops 26214400 | bytes 21401600 | tf_op jit(solution)/shard_map/div | solution.py:86
  51.4 5.2 %reshape.117 = f32[16,4,16,4,256]{4,3,2,1,0:T(4,128)} reshape(f32[64,64,256]{2,1,0:T(8,128)} %get-tuple-element.9) | data formatting | bytes 8388608 | tf_op jit(solution)/shard_map/reshape | solution.py:94
  56.6 3.5 %reduce_sum.18 = f32[16,16,256]{2,1,0:T(8,128)S(1)} reduce(f32[16,4,16,4,256]{4,3,2,1,0:T(4,128)} %reshape.117, f32[]{:T(128)} %constant.109.clone.1), dimensions={1,3}, to_apply=%region_0.1 | reduce | flops 983040 | bytes 4456452 | tf_op jit(solution)/shard_map/reduce_sum | solution.py:94
  60.4 0.8 reshape.129
  61.2 3.9 %all-to-all-start = ((f32[2,1,8192]{2,1,0:T(1,128)}), f32[2,1,8192]{2,1,0:T(1,128)S(1)}, u32[]{:S(2)}, u32[]{:S(2)}) async-start(f32[2,1,8192]{2,1,0:T(1,128)} %reshape.129), calls=%async_computation | async-start | bytes 131072 | tf_op jit(solution)/shard_map/all_to_all | solution.py:103
  65.1 4.4 %all-to-all-done = f32[2,1,8192]{2,1,0:T(1,128)S(1)} async-done(((f32[2,1,8192]{2,1,0:T(1,128)}), f32[2,1,8192]{2,1,0:T(1,128)S(1)}, u32[]{:S(2)}, u32[]{:S(2)}) %all-to-all-start) | async-done | bytes 65568 | tf_op jit(solution)/shard_map/all_to_all | solution.py:103
  70.1 0.8 reduce
  72.0 0.9 reshape.131
  72.9 5.1 %all-to-all-start.1 = ((f32[8,1,2048]{2,1,0:T(1,128)}), f32[8,1,2048]{2,1,0:T(1,128)S(1)}, u32[]{:S(2)}, u32[]{:S(2)}) async-start(f32[8,1,2048]{2,1,0:T(1,128)} %reshape.131), calls=%async_computation.1 | async-start | bytes 131072 | tf_op jit(solution)/shard_map/all_to_all | solution.py:105
  78.1 4.8 %all-to-all-done.1 = f32[8,1,2048]{2,1,0:T(1,128)S(1)} async-done(((f32[8,1,2048]{2,1,0:T(1,128)}), f32[8,1,2048]{2,1,0:T(1,128)S(1)}, u32[]{:S(2)}, u32[]{:S(2)}) %all-to-all-start.1) | async-done | bytes 65568 | tf_op jit(solution)/shard_map/all_to_all | solution.py:105
  82.9 0.8 reduce.1
  85.1 0.9 reshape.133
  86.0 3.5 %all-to-all-start.2 = ((f32[16,1,1024]{2,1,0:T(1,128)}), f32[16,1,1024]{2,1,0:T(1,128)S(1)}, u32[]{:S(2)}, u32[]{:S(2)}) async-start(f32[16,1,1024]{2,1,0:T(1,128)} %reshape.133), calls=%async_computation.2 | async-start | bytes 131072 | tf_op jit(solution)/shard_map/all_to_all | solution.py:107
  89.5 6.6 %all-to-all-done.2 = f32[16,1,1024]{2,1,0:T(1,128)S(1)} async-done(((f32[16,1,1024]{2,1,0:T(1,128)}), f32[16,1,1024]{2,1,0:T(1,128)S(1)}, u32[]{:S(2)}, u32[]{:S(2)}) %all-to-all-start.2) | async-done | bytes 65568 | tf_op jit(solution)/shard_map/all_to_all | solution.py:107
  96.1 0.8 reduce.2
  98.8 0.9 reshape.135
  99.6 3.5 %all-to-all-start.3 = ((f32[16,1,1024]{2,1,0:T(1,128)}), f32[16,1,1024]{2,1,0:T(1,128)S(1)}, u32[]{:S(2)}, u32[]{:S(2)}) async-start(f32[16,1,1024]{2,1,0:T(1,128)} %reshape.135), calls=%async_computation.3 | async-start | bytes 131072 | tf_op jit(solution)/shard_map/all_to_all | solution.py:123
  103.1 4.4 %fusion.99 = (f32[64,64,1]{2,1,0:T(8,128)}, f32[64,64,1]{2,1,0:T(8,128)S(1)}) fusion(f32[64,64,256]{2,1,0:T(8,128)} %get-tuple-element.8), kind=kLoop, calls=%fused_computation.171 | loop fusion | bytes 65536 | tf_op jit(solution)/shard_map/slice | solution.py:27
  107.5 2.2 all-to-all-done.3
  109.7 0.8 reduce.3
  111.6 0.9 reshape.137
  112.5 6.4 %all-to-all-start.4 = ((f32[8,1,2048]{2,1,0:T(1,128)}), f32[8,1,2048]{2,1,0:T(1,128)S(1)}, u32[]{:S(2)}, u32[]{:S(2)}) async-start(f32[8,1,2048]{2,1,0:T(1,128)} %reshape.137), calls=%async_computation.4 | async-start | bytes 131072 | tf_op jit(solution)/shard_map/all_to_all | solution.py:125
  118.9 1.3 fusion.101
  120.2 2.3 copy.53
  122.4 0.8 collective-permute-start.10
  123.9 2.3 collective-permute-start.11
  126.9 1.5 collective-permute-start.9
  128.4 0.8 reduce.4
  130.7 0.9 reshape.139
  131.5 3.3 %all-to-all-start.5 = ((f32[2,1,8192]{2,1,0:T(1,128)}), f32[2,1,8192]{2,1,0:T(1,128)S(1)}, u32[]{:S(2)}, u32[]{:S(2)}) async-start(f32[2,1,8192]{2,1,0:T(1,128)} %reshape.139), calls=%async_computation.5 | async-start | bytes 131072 | tf_op jit(solution)/shard_map/all_to_all | solution.py:127
  134.8 0.9 fusion.100
  135.7 0.9 collective-permute-start.6
  137.9 2.1 copy.56
  140.1 0.8 reduce.5
  141.7 3.0 %broadcast_in_dim.2 = f32[16,4,16,4,256]{4,3,2,1,0:T(4,128)} broadcast(f32[16,16,256]{2,1,0:T(8,128)S(1)} %fusion.40), dimensions={0,2,4} | broadcast | bytes 4456448 | tf_op jit(solution)/shard_map/broadcast_in_dim | solution.py:129
  144.7 5.3 %reshape.118 = f32[64,64,256]{2,1,0:T(8,128)} reshape(f32[16,4,16,4,256]{4,3,2,1,0:T(4,128)} %broadcast_in_dim.2) | data formatting | bytes 8388608 | tf_op jit(solution)/shard_map/reshape | solution.py:131
  150.0 22.4 %fusion.14 = f32[64,64,256]{2,1,0:T(8,128)S(1)} fusion(f32[64,64,256]{2,1,0:T(8,128)} %reshape.118, f32[64,64,256]{2,1,0:T(8,128)} %param.3, f32[64,64,256]{2,1,0:T(8,128)} %get-tuple-element.9, f32[64,64,1]{2,1,0:T(8,128)} %copy.56, f32[66,1,256]{2,1,0:T(1,128)S(1)} %pad.42, f32[66,1,256]{2,1,0:T(1,128)S(1)} %pad.43, ...), kind=kLoop, calls=%fused_computation.33 | loop fusion | flops 34603008 | bytes 21270528 | tf_op jit(solution)/shard_map/add | solution.py:132
  172.5 1.4 collective-permute-start.14
  174.2 3.0 %collective-permute-start.12 = (f32[1,64,256]{2,1,0:T(8,128)S(1)}, f32[1,64,256]{2,1,0:T(8,128)S(1)}, u32[]{:S(2)}, u32[]{:S(2)}) collective-permute-start(f32[1,64,256]{2,1,0:T(8,128)S(1)} %get-tuple-element.15), channel_id=1, source_target_pairs={{16,0},{32,16},{48,32},{64,48},{80,64},{96,80},{112,96},{0,112},{1... | collective-permute-start | bytes 196616 | tf_op jit(solution)/shard_map/ppermute | solution.py:30
  177.2 2.1 fusion.96
  179.3 2.3 copy.71
  181.6 3.6 %collective-permute-start.16 = (f32[64,64,1]{1,0,2:T(8,128)S(1)}, f32[64,64,1]{1,0,2:T(8,128)S(1)}, u32[]{:S(2)}, u32[]{:S(2)}) collective-permute-start(f32[64,64,1]{1,0,2:T(8,128)S(1)} %copy.71), channel_id=1, source_target_pairs={{1,0},{0,1},{3,2},{2,3},{5,4},{4,5},{7,6},{6,7},{9,8},{8,9},{11,10... | collective-permute-start | bytes 49160 | tf_op jit(solution)/shard_map/ppermute | solution.py:30
  186.5 3.0 %collective-permute-start.17 = (f32[64,64,1]{1,0,2:T(8,128)S(1)}, f32[64,64,1]{1,0,2:T(8,128)S(1)}, u32[]{:S(2)}, u32[]{:S(2)}) collective-permute-start(f32[64,64,1]{1,0,2:T(8,128)S(1)} %copy.73), channel_id=1, source_target_pairs={{0,1},{1,0},{2,3},{3,2},{4,5},{5,4},{6,7},{7,6},{8,9},{9,8},{10,11... | collective-permute-start | bytes 49160 | tf_op jit(solution)/shard_map/ppermute | solution.py:29
  189.5 0.7 copy.72
  190.8 2.0 copy.74
  193.0 24.7 %multiply_reduce_fusion = (f32[]{:T(128)}, f32[64,64,256]{2,1,0:T(8,128)}) fusion(f32[64,64,256]{2,1,0:T(8,128)} %param.2, f32[66,1,256]{2,1,0:T(1,128)S(1)} %pad.46, f32[1,64,256]{2,1,0:T(8,128)S(1)} %collective-permute-done.12, f32[64,64,256]{2,1,0:T(8,128)} %copy-done.1, f32[1,64,256]{2,1,0:T(8,128)S(1)} %collective-permute-done.13, ...), kind=kLoop, calls=%fused_computation.77 | loop fusion | flops 35651584 | bytes 12881924 | tf_op jit(solution)/shard_map/reduce_sum | solution.py:135
  217.7 6.9 %psum.35 = f32[]{:T(128)} all-reduce(f32[]{:T(128)} %get-tuple-element.6), channel_id=1, replica_groups=mesh['gx_0'=4,'gx_1'=2,'gy_0'=4,'gy_1'=2,'gz'=2] {'gx_0'}, use_global_device_ids=true, to_apply=%region_2.3 | all-reduce | flops 1 | bytes 8 | tf_op jit(solution)/shard_map/psum | solution.py:42
  224.6 5.9 %psum.36 = f32[]{:T(128)} all-reduce(f32[]{:T(128)} %psum.35), channel_id=1, replica_groups=mesh['gx_0'=4,'gx_1'=2,'gy_0'=4,'gy_1'=2,'gz'=2] {'gx_1'}, use_global_device_ids=true, to_apply=%region_3.4 | all-reduce | flops 1 | bytes 8 | tf_op jit(solution)/shard_map/psum | solution.py:42
  230.5 11.3 %psum.37 = f32[]{:T(128)} all-reduce(f32[]{:T(128)} %psum.36), channel_id=1, replica_groups=mesh['gx_0'=4,'gx_1'=2,'gy_0'=4,'gy_1'=2,'gz'=2] {'gy_0'}, use_global_device_ids=true, to_apply=%region_4.5 | all-reduce | flops 1 | bytes 8 | tf_op jit(solution)/shard_map/psum | solution.py:42
  241.8 8.0 %psum.38 = f32[]{:T(128)} all-reduce(f32[]{:T(128)} %psum.37), channel_id=1, replica_groups=mesh['gx_0'=4,'gx_1'=2,'gy_0'=4,'gy_1'=2,'gz'=2] {'gy_1'}, use_global_device_ids=true, to_apply=%region_5.6 | all-reduce | flops 1 | bytes 8 | tf_op jit(solution)/shard_map/psum | solution.py:42
  249.8 6.5 %psum.39 = f32[]{:T(128)} all-reduce(f32[]{:T(128)} %psum.38), channel_id=1, replica_groups=mesh['gx_0'=4,'gx_1'=2,'gy_0'=4,'gy_1'=2,'gz'=2] {'gz'}, use_global_device_ids=true, to_apply=%region_6.7 | all-reduce | flops 1 | bytes 8 | tf_op jit(solution)/shard_map/psum | solution.py:42
  (84 shorter events, 16.6 us)
Async XLA Ops:
  1.5 25.2 %collective-permute-start.1 = (f32[1,64,256]{2,1,0:T(8,128)S(1)}, f32[1,64,256]{2,1,0:T(8,128)S(1)}, u32[]{:S(2)}, u32[]{:S(2)}) collective-permute-start(f32[1,64,256]{2,1,0:T(8,128)S(1)} %get-tuple-element.27), channel_id=1, source_target_pairs={{0,16},{16,32},{32,48},{48,64},{64,80},{80,96},{96,112},{112,0},{1... | collective-permute-start | bytes 196616 | tf_op jit(solution)/shard_map/ppermute | solution.py:29
  3.7 28.5 %collective-permute-start = (f32[1,64,256]{2,1,0:T(8,128)S(1)}, f32[1,64,256]{2,1,0:T(8,128)S(1)}, u32[]{:S(2)}, u32[]{:S(2)}) collective-permute-start(f32[1,64,256]{2,1,0:T(8,128)S(1)} %get-tuple-element.26), channel_id=1, source_target_pairs={{16,0},{32,16},{48,32},{64,48},{80,64},{96,80},{112,96},{0,112},{1... | collective-permute-start | bytes 196616 | tf_op jit(solution)/shard_map/ppermute | solution.py:30
  13.9 8.9 %collective-permute-start.4 = (f32[64,64,1]{1,0,2:T(8,128)S(1)}, f32[64,64,1]{1,0,2:T(8,128)S(1)}, u32[]{:S(2)}, u32[]{:S(2)}) collective-permute-start(f32[64,64,1]{1,0,2:T(8,128)S(1)} %copy.76), channel_id=1, source_target_pairs={{1,0},{0,1},{3,2},{2,3},{5,4},{4,5},{7,6},{6,7},{9,8},{8,9},{11,10... | collective-permute-start | bytes 49160 | tf_op jit(solution)/shard_map/ppermute | solution.py:30
  17.9 6.8 %collective-permute-start.5 = (f32[64,64,1]{1,0,2:T(8,128)}, f32[64,64,1]{1,0,2:T(8,128)S(1)}, u32[]{:S(2)}, u32[]{:S(2)}) collective-permute-start(f32[64,64,1]{1,0,2:T(8,128)} %copy.77), channel_id=1, source_target_pairs={{0,1},{1,0},{2,3},{3,2},{4,5},{5,4},{6,7},{7,6},{8,9},{9,8},{10,11... | collective-permute-start | bytes 49160 | tf_op jit(solution)/shard_map/ppermute | solution.py:29
  20.2 11.9 %collective-permute-start.2 = (f32[64,1,256]{2,1,0:T(1,128)}, f32[64,1,256]{2,1,0:T(1,128)S(1)}, u32[]{:S(2)}, u32[]{:S(2)}) collective-permute-start(f32[64,1,256]{2,1,0:T(1,128)} %get-tuple-element.25), channel_id=1, source_target_pairs={{2,0},{4,2},{6,4},{8,6},{10,8},{12,10},{14,12},{0,14},{3,1},{5,3},... | collective-permute-start | bytes 196616 | tf_op jit(solution)/shard_map/ppermute | solution.py:30
  22.9 9.3 %collective-permute-start.3 = (f32[64,1,256]{2,1,0:T(1,128)}, f32[64,1,256]{2,1,0:T(1,128)S(1)}, u32[]{:S(2)}, u32[]{:S(2)}) collective-permute-start(f32[64,1,256]{2,1,0:T(1,128)} %get-tuple-element.24), channel_id=1, source_target_pairs={{0,2},{2,4},{4,6},{6,8},{8,10},{10,12},{12,14},{14,0},{1,3},{3,5},... | collective-permute-start | bytes 196616 | tf_op jit(solution)/shard_map/ppermute | solution.py:29
  27.3 5.5 %copy-start = (f32[64,64,256]{2,1,0:T(8,128)S(1)}, f32[64,64,256]{2,1,0:T(8,128)}, u32[]{:S(2)}) copy-start(f32[64,64,256]{2,1,0:T(8,128)} %param.3) | copy-start | bytes 12582916
  56.6 3.6 %copy-start.2 = (s32[256]{0:T(256)S(1)}, s32[256]{0:T(256)}, u32[]{:S(2)}) copy-start(s32[256]{0:T(256)} %and_select_fusion.3) | copy-start | bytes 3076
  56.6 21.4 %copy-start.3 = (f32[128]{0:T(128)S(1)}, f32[128]{0:T(128)}, u32[]{:S(2)}) copy-start(f32[128]{0:T(128)} %fusion.55) | copy-start | bytes 1540
  61.2 8.4 %all-to-all-start = ((f32[2,1,8192]{2,1,0:T(1,128)}), f32[2,1,8192]{2,1,0:T(1,128)S(1)}, u32[]{:S(2)}, u32[]{:S(2)}) async-start(f32[2,1,8192]{2,1,0:T(1,128)} %reshape.129), calls=%async_computation | async-start | bytes 131072 | tf_op jit(solution)/shard_map/all_to_all | solution.py:103
  72.9 10.0 %all-to-all-start.1 = ((f32[8,1,2048]{2,1,0:T(1,128)}), f32[8,1,2048]{2,1,0:T(1,128)S(1)}, u32[]{:S(2)}, u32[]{:S(2)}) async-start(f32[8,1,2048]{2,1,0:T(1,128)} %reshape.131), calls=%async_computation.1 | async-start | bytes 131072 | tf_op jit(solution)/shard_map/all_to_all | solution.py:105
  86.0 10.1 %all-to-all-start.2 = ((f32[16,1,1024]{2,1,0:T(1,128)}), f32[16,1,1024]{2,1,0:T(1,128)S(1)}, u32[]{:S(2)}, u32[]{:S(2)}) async-start(f32[16,1,1024]{2,1,0:T(1,128)} %reshape.133), calls=%async_computation.2 | async-start | bytes 131072 | tf_op jit(solution)/shard_map/all_to_all | solution.py:107
  99.6 10.1 %all-to-all-start.3 = ((f32[16,1,1024]{2,1,0:T(1,128)}), f32[16,1,1024]{2,1,0:T(1,128)S(1)}, u32[]{:S(2)}, u32[]{:S(2)}) async-start(f32[16,1,1024]{2,1,0:T(1,128)} %reshape.135), calls=%async_computation.3 | async-start | bytes 131072 | tf_op jit(solution)/shard_map/all_to_all | solution.py:123
  112.5 15.9 %all-to-all-start.4 = ((f32[8,1,2048]{2,1,0:T(1,128)}), f32[8,1,2048]{2,1,0:T(1,128)S(1)}, u32[]{:S(2)}, u32[]{:S(2)}) async-start(f32[8,1,2048]{2,1,0:T(1,128)} %reshape.137), calls=%async_computation.4 | async-start | bytes 131072 | tf_op jit(solution)/shard_map/all_to_all | solution.py:125
  122.4 14.2 %collective-permute-start.10 = (f32[64,64,1]{1,0,2:T(8,128)S(1)}, f32[64,64,1]{1,0,2:T(8,128)S(1)}, u32[]{:S(2)}, u32[]{:S(2)}) collective-permute-start(f32[64,64,1]{1,0,2:T(8,128)S(1)} %copy.53), channel_id=1, source_target_pairs={{1,0},{0,1},{3,2},{2,3},{5,4},{4,5},{7,6},{6,7},{9,8},{8,9},{11,10... | collective-permute-start | bytes 49160 | tf_op jit(solution)/shard_map/ppermute | solution.py:30
  123.9 14.0 %collective-permute-start.11 = (f32[64,64,1]{1,0,2:T(8,128)S(1)}, f32[64,64,1]{1,0,2:T(8,128)S(1)}, u32[]{:S(2)}, u32[]{:S(2)}) collective-permute-start(f32[64,64,1]{1,0,2:T(8,128)S(1)} %copy.55), channel_id=1, source_target_pairs={{0,1},{1,0},{2,3},{3,2},{4,5},{5,4},{6,7},{7,6},{8,9},{9,8},{10,11... | collective-permute-start | bytes 49160 | tf_op jit(solution)/shard_map/ppermute | solution.py:29
  126.2 13.8 %collective-permute-start.8 = (f32[64,1,256]{2,1,0:T(1,128)S(1)}, f32[64,1,256]{2,1,0:T(1,128)S(1)}, u32[]{:S(2)}, u32[]{:S(2)}) collective-permute-start(f32[64,1,256]{2,1,0:T(1,128)S(1)} %get-tuple-element.21), channel_id=1, source_target_pairs={{2,0},{4,2},{6,4},{8,6},{10,8},{12,10},{14,12},{0,14},{3,1},{5,3},... | collective-permute-start | bytes 196616 | tf_op jit(solution)/shard_map/ppermute | solution.py:30
  126.9 13.2 %collective-permute-start.9 = (f32[64,1,256]{2,1,0:T(1,128)S(1)}, f32[64,1,256]{2,1,0:T(1,128)S(1)}, u32[]{:S(2)}, u32[]{:S(2)}) collective-permute-start(f32[64,1,256]{2,1,0:T(1,128)S(1)} %get-tuple-element.20), channel_id=1, source_target_pairs={{0,2},{2,4},{4,6},{6,8},{8,10},{10,12},{12,14},{14,0},{1,3},{3,5},... | collective-permute-start | bytes 196616 | tf_op jit(solution)/shard_map/ppermute | solution.py:29
  131.5 8.6 %all-to-all-start.5 = ((f32[2,1,8192]{2,1,0:T(1,128)}), f32[2,1,8192]{2,1,0:T(1,128)S(1)}, u32[]{:S(2)}, u32[]{:S(2)}) async-start(f32[2,1,8192]{2,1,0:T(1,128)} %reshape.139), calls=%async_computation.5 | async-start | bytes 131072 | tf_op jit(solution)/shard_map/all_to_all | solution.py:127
  135.7 14.2 %collective-permute-start.6 = (f32[1,64,256]{2,1,0:T(8,128)S(1)}, f32[1,64,256]{2,1,0:T(8,128)S(1)}, u32[]{:S(2)}, u32[]{:S(2)}) collective-permute-start(f32[1,64,256]{2,1,0:T(8,128)S(1)} %get-tuple-element.19), channel_id=1, source_target_pairs={{16,0},{32,16},{48,32},{64,48},{80,64},{96,80},{112,96},{0,112},{1... | collective-permute-start | bytes 196616 | tf_op jit(solution)/shard_map/ppermute | solution.py:30
  136.7 13.3 %collective-permute-start.7 = (f32[1,64,256]{2,1,0:T(8,128)S(1)}, f32[1,64,256]{2,1,0:T(8,128)S(1)}, u32[]{:S(2)}, u32[]{:S(2)}) collective-permute-start(f32[1,64,256]{2,1,0:T(8,128)S(1)} %get-tuple-element.18), channel_id=1, source_target_pairs={{0,16},{16,32},{32,48},{48,64},{64,80},{80,96},{96,112},{112,0},{1... | collective-permute-start | bytes 196616 | tf_op jit(solution)/shard_map/ppermute | solution.py:29
  172.3 7.0 %copy-start.1 = (f32[64,64,256]{2,1,0:T(8,128)}, f32[64,64,256]{2,1,0:T(8,128)S(1)}, u32[]{:S(2)}) copy-start(f32[64,64,256]{2,1,0:T(8,128)S(1)} %fusion.14) | copy-start | bytes 12582916
  172.5 20.4 %collective-permute-start.14 = (f32[64,1,256]{2,1,0:T(1,128)S(1)}, f32[64,1,256]{2,1,0:T(1,128)S(1)}, u32[]{:S(2)}, u32[]{:S(2)}) collective-permute-start(f32[64,1,256]{2,1,0:T(1,128)S(1)} %get-tuple-element.13), channel_id=1, source_target_pairs={{2,0},{4,2},{6,4},{8,6},{10,8},{12,10},{14,12},{0,14},{3,1},{5,3},... | collective-permute-start | bytes 196616 | tf_op jit(solution)/shard_map/ppermute | solution.py:30
  173.8 19.0 %collective-permute-start.15 = (f32[64,1,256]{2,1,0:T(1,128)S(1)}, f32[64,1,256]{2,1,0:T(1,128)S(1)}, u32[]{:S(2)}, u32[]{:S(2)}) collective-permute-start(f32[64,1,256]{2,1,0:T(1,128)S(1)} %get-tuple-element.12), channel_id=1, source_target_pairs={{0,2},{2,4},{4,6},{6,8},{8,10},{10,12},{12,14},{14,0},{1,3},{3,5},... | collective-permute-start | bytes 196616 | tf_op jit(solution)/shard_map/ppermute | solution.py:29
  174.2 18.7 %collective-permute-start.12 = (f32[1,64,256]{2,1,0:T(8,128)S(1)}, f32[1,64,256]{2,1,0:T(8,128)S(1)}, u32[]{:S(2)}, u32[]{:S(2)}) collective-permute-start(f32[1,64,256]{2,1,0:T(8,128)S(1)} %get-tuple-element.15), channel_id=1, source_target_pairs={{16,0},{32,16},{48,32},{64,48},{80,64},{96,80},{112,96},{0,112},{1... | collective-permute-start | bytes 196616 | tf_op jit(solution)/shard_map/ppermute | solution.py:30
  177.2 15.7 %collective-permute-start.13 = (f32[1,64,256]{2,1,0:T(8,128)S(1)}, f32[1,64,256]{2,1,0:T(8,128)S(1)}, u32[]{:S(2)}, u32[]{:S(2)}) collective-permute-start(f32[1,64,256]{2,1,0:T(8,128)S(1)} %get-tuple-element.14), channel_id=1, source_target_pairs={{0,16},{16,32},{32,48},{48,64},{64,80},{80,96},{96,112},{112,0},{1... | collective-permute-start | bytes 196616 | tf_op jit(solution)/shard_map/ppermute | solution.py:29
  181.6 4.9 %collective-permute-start.16 = (f32[64,64,1]{1,0,2:T(8,128)S(1)}, f32[64,64,1]{1,0,2:T(8,128)S(1)}, u32[]{:S(2)}, u32[]{:S(2)}) collective-permute-start(f32[64,64,1]{1,0,2:T(8,128)S(1)} %copy.71), channel_id=1, source_target_pairs={{1,0},{0,1},{3,2},{2,3},{5,4},{4,5},{7,6},{6,7},{9,8},{8,9},{11,10... | collective-permute-start | bytes 49160 | tf_op jit(solution)/shard_map/ppermute | solution.py:30
  186.5 4.3 %collective-permute-start.17 = (f32[64,64,1]{1,0,2:T(8,128)S(1)}, f32[64,64,1]{1,0,2:T(8,128)S(1)}, u32[]{:S(2)}, u32[]{:S(2)}) collective-permute-start(f32[64,64,1]{1,0,2:T(8,128)S(1)} %copy.73), channel_id=1, source_target_pairs={{0,1},{1,0},{2,3},{3,2},{4,5},{5,4},{6,7},{7,6},{8,9},{9,8},{10,11... | collective-permute-start | bytes 49160 | tf_op jit(solution)/shard_map/ppermute | solution.py:29
where the time goes:
time: 260 us; the launch traced here: 258 us
  other arithmetic  75.5 us (29%)
  local copies, waits for them, and re-layouts  63.3 us (24%)
  starting transfers between devices  55.2 us (21%)
  blocking collectives  38.6 us (15%)
  waiting for transfers between devices  19.2 us (7%)
  matrix products  3.43 us (1%)
  between operations  2.93 us (1%)
    psum x5, blocking collectives, over_axes(): return functools.reduce(lax.psum, axes, shard)  38.6 us
    reduce_sum x1, other arithmetic, per_device(): total = over_axes(jnp.sum(new_residual * new_residual), GX_GY_GZ)  24.7 us
    add x1, other arithmetic, per_device(): updated = guess + local_fix + prolonged  22.4 us
    div x1, other arithmetic, per_device(): first_sweep = residual_now / diag_value  18.6 us
    ppermute x9, starting transfers between devices, with_halo(): lax.ppermute(leading, axis, [(b, a) for a, b in up])  18.2 us
    slice x6, local copies, waits for them, and re-layouts, with_halo(): leading = lax.slice_in_dim(shard, 0, width, axis=dim)  16.3 us
    unnamed x24, local copies, waits for them, and re-layouts  15.2 us
    ppermute x9, starting transfers between devices, with_halo(): lax.ppermute(last, axis, up)  11.4 us
  transfers between devices with their start and end apart: 24, of which 6 were waited for; matrix products, arithmetic and copies ran while one was open for 20% of the time, Pallas kernels for 0%

commit v1 on v0

v1 whole, which is shorter than its diff:
```python
import functools

import jax
import jax.numpy as jnp
import numpy as np
from jax import lax
from jax.experimental import pallas as pl
from jax.experimental.pallas import tpu as pltpu
from jax.sharding import PartitionSpec as P

F32 = jnp.float32
MESH = pl.DeviceIdType.MESH
HIGHEST = lax.Precision.HIGHEST

SCREEN = 0.002
DIAG = 6.0 + SCREEN
INV_DIAG = 1.0 / DIAG

BX, BY, BZ = 64, 64, 256
CX, CY, CZ = 16, 16, 64
NC = 128
GX, GY, GZ = 8, 8, 2
GROUP = GY * GZ
KZ = NC // GROUP
ROWS = 24
CHUNKS = 8
PLANES = BX // CHUNKS


def tables():
    def cas(k, n):
        angle = 2.0 * np.pi * ((k * n) % NC) / NC
        return np.cos(angle) + np.sin(angle)

    mode = np.arange(NC)
    z = np.arange(BZ)
    forward_z = np.zeros((GZ, 2 * BZ, NC))
    inverse_z = np.zeros((GZ, NC, 3 * 128))
    for b in range(GZ):
        cell = CZ * b + z // 4
        here = cas(cell[:, None], mode[None, :])
        before = cas(cell[:, None] - 1, mode[None, :])
        after = cas(cell[:, None] + 1, mode[None, :])
        forward_z[b, :BZ] = here
        forward_z[b, BZ:] = np.where((z % 4 == 0)[:, None], before - here, 0.0) + np.where(
            (z % 4 == 3)[:, None], after - here, 0.0
        )
        inverse_z[b, :, :BZ] = here.T
        inverse_z[b, :, BZ] = cas(CZ * b - 1, mode)
        inverse_z[b, :, 3 * 128 - 1] = cas(CZ * b + CZ, mode)
    forward_y = np.zeros((NC, GY * ROWS))
    for b in range(GY):
        place = np.concatenate([CY * b + np.arange(CY), [CY * b - 1, CY * b + CY]])
        forward_y[:, ROWS * b : ROWS * b + CY + 2] = cas(mode[:, None], place[None, :])
    plain_y = cas(mode[:, None], mode[None, :])
    wave = 2.0 - 2.0 * np.cos(2.0 * np.pi * mode / NC)
    wave_y = np.broadcast_to(wave[:, None], (NC, NC))
    wave_z = np.tile(wave.reshape(GROUP, 1, KZ), (1, CX, 1)).reshape(GROUP, NC)
    out = (forward_z, inverse_z, forward_y, forward_y.T, plain_y, wave_y, wave_z)
    return tuple(np.ascontiguousarray(t, dtype=np.float32) for t in out)


def dot(a, b):
    return jnp.dot(a, b, precision=HIGHEST, preferred_element_type=F32)


def iota(shape, dim):
    return lax.broadcasted_iota(jnp.int32, shape, dim)


def neighbour_sum(a, below, above, row_low, row_high, edge):
    rows, lanes = iota(a.shape, 0), iota(a.shape, 1)
    edges = jnp.concatenate([edge, edge], axis=1)
    total = below + above
    total = total + jnp.where(rows == 0, row_low, pltpu.roll(a, 1, 0))
    total = total + jnp.where(rows == BY - 1, row_high, pltpu.roll(a, BY - 1, 0))
    total = total + jnp.where(lanes == 0, edges, pltpu.roll(a, 1, 1))
    total = total + jnp.where(lanes == BZ - 1, edges, pltpu.roll(a, BZ - 1, 1))
    return total


def pack_edges(a, x, held):
    lane = iota((BY, 128), 1)
    held = jnp.where(lane == x, pltpu.roll(a[:, 128:], x + 1, 1), held)
    return jnp.where(lane == BX + x, pltpu.roll(a[:, :128], BX + x, 1), held)


def unpack_edges(held, x):
    lane = iota((BY, 128), 1)
    low = pltpu.roll(held, lax.rem(128 - x, 128), 1)
    return jnp.where(lane == 0, low, pltpu.roll(held, 63 - x, 1))


def spread_lanes(a):
    a = jnp.where(iota(a.shape, 1) < KZ, a, 0.0)
    for shift in (8, 16, 32, 64):
        a = a + pltpu.roll(a, shift, 1)
    return a


def exchange_kernel(
    rs_hbm, g_hbm, fz_hbm, fy_hbm, iy_hbm, py_hbm, wy_hbm, wz_hbm,
    w_hbm, wx_hbm, wyh_hbm, wzh_hbm, c_hbm,
    g, rs, res, w, fz, fy, iy, py, wy, wz,
    fold, folded, spec, a_send, a_recv, m_send, m_recv, c_send, c_recv,
    y_send, y_recv, z_send, z_recv,
    g_sem, rs_sem, t_sem, out_sem,
    x_ss, x_rs, y_ss, y_rs, z_ss, z_rs, a_ss, a_rs, m_ss, m_rs, c_ss, c_rs, own_sem,
):
    bx, by, bz = lax.axis_index("gx"), lax.axis_index("gy"), lax.axis_index("gz")
    me = bz * GY + by

    barrier = pltpu.get_barrier_semaphore()

    def greet_group(d, _):
        peer = lax.rem(me + d, GROUP)
        pl.semaphore_signal(
            barrier, inc=1, device_id={"gy": lax.rem(peer, GY), "gz": peer // GY}, device_id_type=MESH
        )
        return _

    def greet_line(d, _):
        pl.semaphore_signal(barrier, inc=1, device_id={"gx": lax.rem(bx + d, GX)}, device_id_type=MESH)
        return _

    lax.fori_loop(1, GX, greet_line, 0)
    lax.fori_loop(1, GROUP, greet_group, 0)

    loads_g, loads_rs = [], []
    for c in range(CHUNKS):
        part = pl.ds(PLANES * c, PLANES)
        loads_g.append(
            pltpu.make_async_copy(g_hbm.at[part], g.at[pl.ds(PLANES * c + 1, PLANES)], g_sem.at[c])
        )
        loads_rs.append(pltpu.make_async_copy(rs_hbm.at[part], rs.at[part], rs_sem.at[c]))
    loads_t = [
        pltpu.make_async_copy(src, dst, t_sem.at[i])
        for i, (src, dst) in enumerate(
            ((fz_hbm.at[bz], fz), (fy_hbm, fy), (iy_hbm, iy), (py_hbm, py), (wy_hbm, wy), (wz_hbm, wz))
        )
    ]
    for c in range(CHUNKS):
        loads_g[c].start()
        loads_rs[c].start()
    for load in loads_t:
        load.start()

    pl.semaphore_wait(barrier, GX - 1 + GROUP - 1)

    up_x, down_x = lax.rem(bx + 1, GX), lax.rem(bx + GX - 1, GX)
    up_y, down_y = lax.rem(by + 1, GY), lax.rem(by + GY - 1, GY)

    def planes_out(phase, first, last, array):
        return [
            pltpu.make_async_remote_copy(
                first, array.at[BX + 1], x_ss.at[phase, 0], x_rs.at[phase, 0],
                device_id={"gx": down_x}, device_id_type=MESH,
            ),
            pltpu.make_async_remote_copy(
                last, array.at[0], x_ss.at[phase, 1], x_rs.at[phase, 1],
                device_id={"gx": up_x}, device_id_type=MESH,
            ),
        ]

    def edges_out(phase):
        return [
            pltpu.make_async_remote_copy(
                y_send.at[phase, 0], y_recv.at[phase, 1], y_ss.at[phase, 0], y_rs.at[phase, 0],
                device_id={"gy": down_y}, device_id_type=MESH,
            ),
            pltpu.make_async_remote_copy(
                y_send.at[phase, 1], y_recv.at[phase, 0], y_ss.at[phase, 1], y_rs.at[phase, 1],
                device_id={"gy": up_y}, device_id_type=MESH,
            ),
            pltpu.make_async_remote_copy(
                z_send.at[phase], z_recv.at[phase], z_ss.at[phase], z_rs.at[phase],
                device_id={"gz": 1 - bz}, device_id_type=MESH,
            ),
        ]

    g_planes = planes_out(0, g_hbm.at[0], g_hbm.at[BX - 1], g)
    for copy in g_planes:
        copy.start()

    folded[:, CY:, :] = jnp.zeros((CX, ROWS - CY, 2 * BZ), F32)

    def fold_plane(X, _):
        x = 4 * X + 1
        first, last = g[x], g[x + 3]
        plane = first + g[x + 1] + g[x + 2] + last
        rest = rs[x - 1] + rs[x] + rs[x + 1] + rs[x + 2] - SCREEN * plane
        rest = rest + (g[x - 1] - first) + (g[x + 4] - last)
        rows = iota((CY, 128), 0)
        for half in range(2):
            lanes = slice(128 * half, 128 * (half + 1))
            fold[half] = rest[:, lanes]
            fold[2 + half] = plane[:, lanes]
            a0, a1, a2, a3 = [fold[2 + half, pl.ds(a, CY, stride=4), :] for a in range(4)]
            e0, e1, e2, e3 = [fold[half, pl.ds(a, CY, stride=4), :] for a in range(4)]
            before = jnp.where(rows == 0, 0.0, pltpu.roll(a3, 1, 0))
            after = jnp.where(rows == CY - 1, 0.0, pltpu.roll(a0, CY - 1, 0))
            folded[X, 0:CY, lanes] = (e0 + e1) + (e2 + e3) + (before - a0) + (after - a3)
            folded[X, 0:CY, BZ + 128 * half : BZ + 128 * (half + 1)] = (a0 + a1) + (a2 + a3)
        folded[X, CY : CY + 1, 0:BZ] = plane[0:1, :]
        folded[X, CY + 1 : CY + 2, 0:BZ] = plane[BY - 1 : BY, :]
        return _

    done = 1
    for c in range(CHUNKS):
        loads_g[c].wait()
        loads_rs[c].wait()
        ready = min(CX - 1, (PLANES * (c + 1) - 1) // 4)
        lax.fori_loop(done, ready, fold_plane, 0)
        done = max(done, ready)
    for copy in g_planes:
        copy.wait_recv()
    lax.fori_loop(0, 2, lambda i, _: fold_plane(i * (CX - 1), _), 0)

    for load in loads_t:
        load.wait()

    def modes(X, _):
        spec[X] = pltpu.roll(dot(folded[X], fz[...]), lax.rem(8 * X, 128), 1)
        return _

    lax.fori_loop(0, CX, modes, 0)

    group = iota((ROWS, 128), 1) // KZ

    def copy_a(t, slot):
        return pltpu.make_async_remote_copy(
            a_send.at[t], a_recv.at[slot], a_ss.at[t], a_rs.at[slot],
            device_id={"gy": lax.rem(t, GY), "gz": t // GY}, device_id_type=MESH,
        )

    def send_a(d, _):
        t = lax.rem(me + d, GROUP)
        out = jnp.zeros((ROWS, 128), F32)
        for X in range(CX):
            out = jnp.where(group == lax.rem(t + X, CX), spec[X], out)
        a_send[t] = out
        copy_a(t, me).start()
        return _

    lax.fori_loop(1, GROUP, send_a, 0)
    own = jnp.zeros((ROWS, 128), F32)
    for X in range(CX):
        own = jnp.where(group == lax.rem(me + X, CX), spec[X], own)
    a_recv[me] = own

    lane64 = iota((BY, 128), 1)

    def pack_plane(phase, x, a, held):
        y_send[phase, 0, pl.ds(x, 1), :] = a[0:1, :]
        y_send[phase, 1, pl.ds(x, 1), :] = a[BY - 1 : BY, :]
        return pack_edges(a, x, held)

    z_send[0] = lax.fori_loop(0, BX, lambda x, h: pack_plane(0, x, g[x + 1], h), jnp.zeros((BY, 128), F32))
    g_edges = edges_out(0)
    for copy in g_edges:
        copy.start()

    place = iota((NC, 128), 1) // KZ
    wave = SCREEN * 16.0 + wy[...] + wz[pl.ds(me, 1), :]
    r = 1.0 / (1.0 + 0.5 * wave + jnp.sqrt(wave + 0.25 * wave * wave))
    r2 = r * r
    r4 = r2 * r2
    r8 = r4 * r4
    r16 = r8 * r8

    for copy in g_edges:
        copy.wait_recv()

    def residual_plane(x, held):
        a = g[x + 1]
        total = neighbour_sum(
            a, g[x], g[x + 2], y_recv[0, 0, pl.ds(x, 1), :], y_recv[0, 1, pl.ds(x, 1), :],
            unpack_edges(z_recv[0], x),
        )
        out = rs[x] - (DIAG * a - total)
        res[x + 1] = out
        return pack_plane(1, x, out, held)

    z_send[1] = lax.fori_loop(0, BX, residual_plane, jnp.zeros((BY, 128), F32))
    res_copies = planes_out(1, res.at[1], res.at[BX], res) + edges_out(1)
    for copy in res_copies:
        copy.start()

    def wait_a(d, _):
        t = lax.rem(me + d, GROUP)
        copy_a(t, t).wait_recv()
        return _

    lax.fori_loop(1, GROUP, wait_a, 0)
    lines = (a_recv[0:GY] + a_recv[GY:GROUP]).reshape(GY * ROWS, 128)
    u = pltpu.roll(dot(fy[...], lines), lax.rem(128 - KZ * me + 128, 128), 1)

    right, left = u, u
    for step, power in ((1, r), (2, r2), (4, r4), (8, r8)):
        right = right + jnp.where(place >= step, power * pltpu.roll(right, KZ * step, 1), 0.0)
        left = left + jnp.where(place < CX - step, power * pltpu.roll(left, 128 - KZ * step, 1), 0.0)
    lane = iota((NC, 128), 1)
    ends = jnp.where(lane < KZ, left, pltpu.roll(right, 2 * KZ, 1))
    slot16 = iota((CX, 128), 1) // (2 * KZ)
    packed = jnp.zeros((CX, 128), F32)
    decay = jnp.zeros((CX, 128), F32)
    for i in range(8):
        part = ends[CX * i : CX * (i + 1)]
        packed = jnp.where(slot16 == i, pltpu.roll(part, 2 * KZ * i, 1) if i else part, packed)
        decay = jnp.where(slot16 == i, r16[CX * i : CX * (i + 1)], decay)
    m_send[...] = packed
    m_recv[0] = packed

    def copy_m(d):
        return pltpu.make_async_remote_copy(
            m_send, m_recv.at[d], m_ss.at[d], m_rs.at[d],
            device_id={"gx": lax.rem(bx + d, GX)}, device_id_type=MESH,
        )

    for d in range(1, GX):
        copy_m(d).start()

    end_left, end_right = spread_lanes(left), spread_lanes(pltpu.roll(right, KZ, 1))
    from_low, from_high = r, r
    for bit, power in ((1, r), (2, r2), (4, r4), (8, r8)):
        has = (place // bit) % 2 == 1
        from_low = from_low * jnp.where(has, power, 1.0)
        from_high = from_high * jnp.where(has, 1.0, power)
    scale = (0.25 / (NC * NC)) * r / (1.0 - r2)
    local = right + left - u
    decay8 = decay * decay
    decay8 = decay8 * decay8
    decay8 = decay8 * decay8
    wrap = 1.0 / (1.0 - decay8)

    for copy in res_copies:
        copy.wait_recv()

    def fix_plane(x, held):
        a = res[x + 1]
        total = neighbour_sum(
            a, res[x], res[x + 2], y_recv[1, 0, pl.ds(x, 1), :], y_recv[1, 1, pl.ds(x, 1), :],
            unpack_edges(z_recv[1], x),
        )
        out = g[x + 1] + (a + total * INV_DIAG) * INV_DIAG
        w[x + 1] = out
        return pack_plane(2, x, out, held)

    z_send[2] = lax.fori_loop(0, BX, fix_plane, jnp.zeros((BY, 128), F32))
    w_copies = planes_out(2, w.at[1], w.at[BX], w) + edges_out(2)
    for copy in w_copies:
        copy.start()
    w_out = pltpu.make_async_copy(w.at[pl.ds(1, BX)], w_hbm, out_sem.at[0])
    w_out.start()

    for d in range(1, GX):
        copy_m(d).wait_recv()
    is_right = (iota((CX, 128), 1) // KZ) % 2 == 1
    incoming = jnp.zeros((CX, 128), F32)
    for d in range(GX, 0, -1):
        incoming = jnp.where(is_right, m_recv[d % GX], m_recv[(GX - d) % GX]) + decay * incoming
    incoming = incoming * wrap
    unpacked = jnp.concatenate(
        [pltpu.roll(incoming, 128 - 2 * KZ * i, 1) if i else incoming for i in range(8)], axis=0
    )
    in_left, in_right = spread_lanes(unpacked), spread_lanes(pltpu.roll(unpacked, 128 - KZ, 1))
    solved = scale * (local + from_low * in_right + from_high * in_left)
    before = scale * (r * end_left + in_right + r16 * (r * in_left))
    after = scale * (r * end_right + in_left + r16 * (r * in_right))

    lines = dot(iy[...], pltpu.roll(solved, KZ * me, 1)).reshape(GY, ROWS, 128)
    diagonal = iota((NC, 128), 0) % CY == place
    low = jnp.where(diagonal, dot(py[...], before), 0.0).reshape(GY, CY, 128).sum(axis=1)
    high = jnp.where(diagonal, dot(py[...], after), 0.0).reshape(GY, CY, 128).sum(axis=1)
    c_send[...] = lines
    for b in range(GY):
        c_send[b, CY + 2 : CY + 3, :] = low[b : b + 1]
        c_send[b, CY + 3 : CY + 4, :] = high[b : b + 1]

    def copy_c(t, slot):
        return pltpu.make_async_remote_copy(
            c_send.at[lax.rem(t, GY)], c_recv.at[slot], c_ss.at[t], c_rs.at[slot],
            device_id={"gy": lax.rem(t, GY), "gz": t // GY}, device_id_type=MESH,
        )

    def send_c(d, _):
        copy_c(lax.rem(me + d, GROUP), me).start()
        return _

    lax.fori_loop(1, GROUP, send_c, 0)
    own_copy = pltpu.make_async_copy(c_send.at[by], c_recv.at[me], own_sem)
    own_copy.start()

    for copy in w_copies:
        copy.wait_recv()
    outs = [
        pltpu.make_async_copy(w.at[0], wx_hbm.at[0], out_sem.at[1]),
        pltpu.make_async_copy(w.at[BX + 1], wx_hbm.at[1], out_sem.at[2]),
        pltpu.make_async_copy(y_recv.at[2], wyh_hbm, out_sem.at[3]),
        pltpu.make_async_copy(z_recv.at[2], wzh_hbm, out_sem.at[4]),
    ]
    for copy in outs:
        copy.start()

    own_copy.wait()

    def wait_c(d, _):
        t = lax.rem(me + d, GROUP)
        copy_c(t, t).wait_recv()
        return _

    lax.fori_loop(1, GROUP, wait_c, 0)
    c_out = pltpu.make_async_copy(c_recv, c_hbm, out_sem.at[5])
    c_out.start()

    for copy in g_planes + g_edges + res_copies + w_copies:
        copy.wait_send()

    def wait_sent(d, _):
        t = lax.rem(me + d, GROUP)
        copy_a(t, t).wait_send()
        copy_c(t, t).wait_send()
        return _

    lax.fori_loop(1, GROUP, wait_sent, 0)
    for d in range(1, GX):
        copy_m(d).wait_send()
    w_out.wait()
    for copy in outs:
        copy.wait()
    c_out.wait()


def final_kernel(
    w_hbm, rs_hbm, wx_hbm, wyh_hbm, wzh_hbm, c_hbm, iz_hbm,
    up_hbm, new_hbm, sum_ref,
    up, rs, new, wyh, wzh, c, iz, basis, corr, ends,
    w_sem, rs_sem, s_sem, up_sem, new_sem,
):
    bz = lax.axis_index("gz")
    small = [
        pltpu.make_async_copy(src, dst, s_sem.at[i])
        for i, (src, dst) in enumerate(
            (
                (c_hbm, c), (iz_hbm.at[bz], iz), (wx_hbm.at[0], up.at[0]), (wx_hbm.at[1], up.at[BX + 1]),
                (wyh_hbm, wyh), (wzh_hbm, wzh),
            )
        )
    ]
    loads_w, loads_rs, stores_up, stores_new = [], [], [], []
    for k in range(CHUNKS):
        part, shifted = pl.ds(PLANES * k, PLANES), pl.ds(PLANES * k + 1, PLANES)
        loads_w.append(pltpu.make_async_copy(w_hbm.at[part], up.at[shifted], w_sem.at[k]))
        loads_rs.append(pltpu.make_async_copy(rs_hbm.at[part], rs.at[part], rs_sem.at[k]))
        stores_up.append(pltpu.make_async_copy(up.at[shifted], up_hbm.at[part], up_sem.at[k]))
        stores_new.append(pltpu.make_async_copy(new.at[part], new_hbm.at[part], new_sem.at[k]))
    for copy in small:
        copy.start()
    for k in range(CHUNKS):
        loads_w[k].start()
        loads_rs[k].start()
    for copy in small:
        copy.wait()

    group = iota((ROWS, 128), 1) // KZ

    def gather(X, _):
        out = jnp.zeros((ROWS, 128), F32)
        for t in range(GROUP):
            out = jnp.where(group == lax.rem(X + t, CX), c[t], out)
        basis[X + 1] = pltpu.roll(out, lax.rem(128 - KZ * X + 128, 128), 1)
        return _

    lax.fori_loop(0, CX, gather, 0)
    row, place = iota((CY, 128), 0), iota((CY, 128), 1) // KZ
    for side, X in ((0, 0), (1, CX + 1)):
        out = jnp.zeros((CY, 128), F32)
        for t in range(GROUP):
            line = jnp.where(row == place, c[t, CY + 2 + side : CY + 3 + side, :], 0.0)
            for shift in (8, 16, 32, 64):
                line = line + pltpu.roll(line, shift, 1)
            out = jnp.where(place == t, line, out)
        basis[X, 0:CY, :] = out
        basis[X, CY:, :] = jnp.zeros((ROWS - CY, 128), F32)

    def prolong(X, _):
        out = dot(basis[X], iz[...])
        for part in range(3):
            for a in range(4):
                corr[X, part, pl.ds(a, CY, stride=4), :] = out[0:CY, 128 * part : 128 * (part + 1)]
        ends[X] = out[CY:ROWS]
        return _

    lax.fori_loop(0, CX + 2, prolong, 0)

    def correct(x, X):
        for half in range(2):
            lanes = slice(128 * half, 128 * (half + 1))
            up[x, :, lanes] = up[x, :, lanes] + corr[X, half]

    correct(0, 0)
    correct(BX + 1, CX + 1)

    def update_plane(x, _):
        correct(x + 1, x // 4 + 1)
        return _

    def residual_plane(x, total):
        X = x // 4 + 1
        a = up[x + 1]
        low = wyh[0, pl.ds(x, 1), :] + ends[X, 0:1, 0:BZ]
        high = wyh[1, pl.ds(x, 1), :] + ends[X, 1:2, 0:BZ]
        edge = unpack_edges(wzh[...], x) + corr[X, 2]
        near = neighbour_sum(a, up[x], up[x + 2], low, high, edge)
        out = rs[x] - (DIAG * a - near)
        new[x] = out
        square = out * out
        square = square[:, :128] + square[:, 128:]
        return total + square.reshape(8, 8, 128).sum(axis=0)

    total = jnp.zeros((8, 128), F32)
    done = 0
    for k in range(CHUNKS):
        loads_w[k].wait()
        loads_rs[k].wait()
        lax.fori_loop(PLANES * k, PLANES * (k + 1), update_plane, 0)
        stores_up[k].start()
        ready = BX if k == CHUNKS - 1 else PLANES * (k + 1) - 1
        total = lax.fori_loop(done, ready, residual_plane, total)
        done = ready
        if k > 0:
            stores_new[k - 1].start()
    stores_new[CHUNKS - 1].start()
    sum_ref[...] = total
    for k in range(CHUNKS):
        stores_up[k].wait()
        stores_new[k].wait()


def norm_kernel(part_ref, out_ref, first, second, held, s1, r1, s2, r2):
    bx, by, bz = lax.axis_index("gx"), lax.axis_index("gy"), lax.axis_index("gz")
    planes = GX * GZ
    me = bz * GX + bx
    barrier = pltpu.get_barrier_semaphore()
    for d in range(1, GY):
        pl.semaphore_signal(barrier, inc=1, device_id={"gy": lax.rem(by + d, GY)}, device_id_type=MESH)

    def greet(d, _):
        t = lax.rem(me + d, planes)
        pl.semaphore_signal(
            barrier, inc=1, device_id={"gx": lax.rem(t, GX), "gz": t // GX}, device_id_type=MESH
        )
        return _

    lax.fori_loop(1, planes, greet, 0)
    pl.semaphore_wait(barrier, GY - 1 + planes - 1)

    def copy_1(t, slot):
        return pltpu.make_async_remote_copy(
            part_ref, first.at[slot], s1.at[t], r1.at[slot], device_id={"gy": t}, device_id_type=MESH
        )

    for d in range(1, GY):
        copy_1(lax.rem(by + d, GY), by).start()
    first[by] = part_ref[...]
    for d in range(1, GY):
        t = lax.rem(by + d, GY)
        copy_1(t, t).wait_recv()
    total = first[0]
    for b in range(1, GY):
        total = total + first[b]
    held[...] = total

    def copy_2(t, slot):
        return pltpu.make_async_remote_copy(
            held, second.at[slot], s2.at[t], r2.at[slot],
            device_id={"gx": lax.rem(t, GX), "gz": t // GX}, device_id_type=MESH,
        )

    def send_2(d, _):
        copy_2(lax.rem(me + d, planes), me).start()
        return _

    lax.fori_loop(1, planes, send_2, 0)
    second[me] = total

    def wait_2(d, _):
        t = lax.rem(me + d, planes)
        copy_2(t, t).wait_recv()
        return _

    lax.fori_loop(1, planes, wait_2, 0)
    total = second[0]
    for b in range(1, planes):
        total = total + second[b]
    out_ref[...] = jnp.sqrt(jnp.full((8, 128), jnp.sum(total), F32))

    def wait_sent(d, _):
        t = lax.rem(me + d, planes)
        copy_2(t, t).wait_send()
        return _

    lax.fori_loop(1, planes, wait_sent, 0)
    for d in range(1, GY):
        t = lax.rem(by + d, GY)
        copy_1(t, t).wait_send()


ANY = pl.BlockSpec(memory_space=pl.ANY)
IN_VMEM = pl.BlockSpec(memory_space=pltpu.VMEM)
DMA = pltpu.SemaphoreType.DMA
VMEM = pltpu.VMEM


def per_device(right_side, guess):
    forward_z, inverse_z, forward_y, back_y, plain_y, wave_y, wave_z = [jnp.asarray(t) for t in tables()]
    shape = jax.ShapeDtypeStruct
    block = (BX, BY, BZ)
    padded = (BX + 2, BY, BZ)
    w, wx, wyh, wzh, c = pl.pallas_call(
        exchange_kernel,
        out_shape=(
            shape(block, F32), shape((2, BY, BZ), F32), shape((2, BX, BZ), F32), shape((BY, 128), F32),
            shape((GROUP, ROWS, 128), F32),
        ),
        in_specs=[ANY] * 8,
        out_specs=(ANY,) * 5,
        scratch_shapes=[
            VMEM(padded, F32), VMEM(block, F32), VMEM(padded, F32), VMEM(padded, F32),
            VMEM((2 * BZ, NC), F32), VMEM((NC, GY * ROWS), F32), VMEM((GY * ROWS, NC), F32),
            VMEM((NC, NC), F32), VMEM((NC, NC), F32), VMEM((GROUP, NC), F32),
            VMEM((4, BY, 128), F32), VMEM((CX, ROWS, 2 * BZ), F32), VMEM((CX, ROWS, 128), F32),
            VMEM((GROUP, ROWS, 128), F32), VMEM((GROUP, ROWS, 128), F32),
            VMEM((CX, 128), F32), VMEM((GX, CX, 128), F32),
            VMEM((GY, ROWS, 128), F32), VMEM((GROUP, ROWS, 128), F32),
            VMEM((3, 2, BX, BZ), F32), VMEM((3, 2, BX, BZ), F32), VMEM((3, BY, 128), F32), VMEM((3, BY, 128), F32),
            DMA((CHUNKS,)), DMA((CHUNKS,)), DMA((6,)), DMA((6,)),
            DMA((3, 2)), DMA((3, 2)), DMA((3, 2)), DMA((3, 2)), DMA((3,)), DMA((3,)),
            DMA((GROUP,)), DMA((GROUP,)), DMA((GX,)), DMA((GX,)), DMA((GROUP,)), DMA((GROUP,)), DMA,
        ],
        compiler_params=pltpu.CompilerParams(
            collective_id=0, has_side_effects=True, vmem_limit_bytes=48 * 1024 * 1024
        ),
        name="exchange",
    )(right_side, guess, forward_z, forward_y, back_y, plain_y, wave_y, wave_z)
    updated, new_residual, part = pl.pallas_call(
        final_kernel,
        out_shape=(shape(block, F32), shape(block, F32), shape((8, 128), F32)),
        in_specs=[ANY] * 7,
        out_specs=(ANY, ANY, IN_VMEM),
        scratch_shapes=[
            VMEM(padded, F32), VMEM(block, F32), VMEM(block, F32),
            VMEM((2, BX, BZ), F32), VMEM((BY, 128), F32), VMEM((GROUP, ROWS, 128), F32),
            VMEM((NC, 3 * 128), F32), VMEM((CX + 2, ROWS, 128), F32),
            VMEM((CX + 2, 3, BY, 128), F32), VMEM((CX + 2, ROWS - CY, 3 * 128), F32),
            DMA((CHUNKS,)), DMA((CHUNKS,)), DMA((6,)), DMA((CHUNKS,)), DMA((CHUNKS,)),
        ],
        compiler_params=pltpu.CompilerParams(vmem_limit_bytes=48 * 1024 * 1024),
        name="final",
    )(w, right_side, wx, wyh, wzh, c, inverse_z)
    norm = pl.pallas_call(
        norm_kernel,
        out_shape=shape((8, 128), F32),
        in_specs=[IN_VMEM],
        out_specs=IN_VMEM,
        scratch_shapes=[
            VMEM((GY, 8, 128), F32), VMEM((GX * GZ, 8, 128), F32), VMEM((8, 128), F32),
            DMA((GY,)), DMA((GY,)), DMA((GX * GZ,)), DMA((GX * GZ,)),
        ],
        compiler_params=pltpu.CompilerParams(collective_id=1, has_side_effects=True),
        name="norm",
    )(part)
    return updated, new_residual, norm[0, 0]


def solution(mesh):
    spec = P("gx", "gy", "gz")
    return jax.shard_map(
        per_device, mesh=mesh, in_specs=(spec, spec), out_specs=(spec, spec, P()), check_vma=False
    )
```

time: 260 us -> 110 us (0.42)
  Pallas kernels: 0 us -> 102 us
  other arithmetic: 75.5 us -> 0 us
  local copies, waits for them, and re-layouts: 63.3 us -> 6.98 us
  starting transfers between devices: 55.2 us -> 0 us
  blocking collectives: 38.6 us -> 0 us
  waiting for transfers between devices: 19.2 us -> 0 us
  matrix products: 3.43 us -> 0 us
    pallas_call x0 -> x3, Pallas kernels: none -> 102 us  [the longest x1 70.3 us: per_device(): pl.pallas_call(exchange_kernel, out_shape=(shape(block, F32), shape((2, B...]
    psum x5 -> x0, blocking collectives: 38.6 us -> none  [over_axes(): return functools.reduce(lax.psum, axes, shard)]
    ppermute x18 -> x0, starting transfers between devices: 29.5 us -> none  [the longest x9 18.2 us: with_halo(): lax.ppermute(leading, axis, [(b, a) for a, b in up])]
    reduce_sum x2 -> x0, other arithmetic: 28.2 us -> none  [the longest x1 24.7 us: per_device(): total = over_axes(jnp.sum(new_residual * new_residual), GX_GY_GZ)]
    all_to_all x6 -> x0, starting transfers between devices: 25.7 us -> none  [the longest x1 6.37 us: per_device(): lax.all_to_all(spectra, GY, split_axis=1, concat_axis=2, tiled=True)]
    add x3 -> x0, other arithmetic: 23 us -> none  [the longest x1 22.4 us: per_device(): updated = guess + local_fix + prolonged]
    slice x13 -> x1, local copies, waits for them, and re-layouts: 21.9 us -> 1.19 us  [per_device(): return (updated, new_residual, norm[0, 0])]
    div x4 -> x0, other arithmetic: 18.8 us -> none  [the longest x1 18.6 us: per_device(): first_sweep = residual_now / diag_value]
  transfers between devices with their start and end apart: 24 -> 0, of which waited for: 6 -> 0; matrix products, arithmetic and copies ran while one was open for 20% -> 0% of each run, Pallas kernels for 0% -> 0%
where the time goes in v1:
time: 110 us
  Pallas kernels  102 us (93%)
  local copies, waits for them, and re-layouts  6.98 us (6%)
    pallas_call x1, Pallas kernels, per_device(): pl.pallas_call(exchange_kernel, out_shape=(shape(block, F32), shape((2, B...  70.3 us
    pallas_call x1, Pallas kernels, per_device(): pl.pallas_call(final_kernel, out_shape=(shape(block, F32), shape(block, F...  18 us
    pallas_call x1, Pallas kernels, per_device(): pl.pallas_call(norm_kernel, out_shape=shape((8, 128), F32), in_specs=[IN_...  13.6 us
    unnamed x16, local copies, waits for them, and re-layouts  5.79 us

profile of v1, /device:TPU:1, one launch (start us, length us, event | category | flops | bytes accessed | tf_op | source)
XLA Modules:
  0.0 109.6 jit_solution(10485422892533636100)
XLA Ops:
  0.6 0.0 copy-start
  0.6 1.0 copy-done
  1.7 0.0 copy-start.2
  1.7 0.9 copy-done.2
  2.6 0.0 copy-start.3
  2.6 0.9 copy-done.3
  3.5 0.0 copy-start.4
  3.5 0.8 copy-done.4
  4.3 0.0 copy-start.5
  4.3 0.8 copy-done.5
  5.2 0.0 copy-start.6
  5.2 0.7 copy-done.6
  5.9 0.0 copy-start.1
  5.9 70.3 %exchange.1 = (f32[64,64,256]{2,1,0:T(8,128)S(1)}, f32[2,64,256]{2,1,0:T(8,128)S(1)}, f32[2,64,256]{2,1,0:T(8,128)S(1)}, f32[64,128]{1,0:T(8,128)S(1)}, f32[16,24,128]{2,1,0:T(8,128)S(1)}) custom-call(f32[64,64,256]{2,1,0:T(8,128)} %rs_hbm.3, f32[64,64,256]{2,1,0:T(8,128)} %g_hbm.1, f32[2,512,128]{2,1,0:T(8,128)S(1)} %copy-done, f32[128,192]{1,0:T(8,128)S(1)} %copy-done.2, ...), custom_call_target="tpu_custom_call" | custom-call | tf_op jit(solution)/shard_map/exchange/pallas_call | solution.py:620
  76.2 0.0 copy-done.1
  76.2 18.0 %final.1 = (f32[64,64,256]{2,1,0:T(8,128)}, f32[64,64,256]{2,1,0:T(8,128)}, f32[8,128]{1,0:T(8,128)S(1)}) custom-call(f32[64,64,256]{2,1,0:T(8,128)S(1)} %get-tuple-element.11.w_hbm, f32[64,64,256]{2,1,0:T(8,128)} %rs_hbm.3, f32[2,64,256]{2,1,0:T(8,128)S(1)} %get-tuple-element.12.wx_hbm, f32[2,64,256]{2,1,0:T(8,128)S(1)} %get-tuple-element.13.wyh_hbm, ...), custom_call_target="tpu_custom_call" | custom-call | tf_op jit(solution)/shard_map/final/pallas_call | solution.py:646
  94.2 0.0 copy-start.7
  94.2 0.6 copy-done.7
  94.8 13.6 %norm.1 = f32[8,128]{1,0:T(8,128)} custom-call(f32[8,128]{1,0:T(8,128)} %copy-done.7), custom_call_target="tpu_custom_call" | custom-call | tf_op jit(solution)/shard_map/norm/pallas_call | solution.py:661
  108.4 1.2 %slice.3 = f32[1,1]{1,0:T(1,128)} slice(f32[8,128]{1,0:T(8,128)} %norm.1), slice={[0:1], [0:1]} | slice | bytes 8 | tf_op jit(solution)/shard_map/slice | solution.py:673
Async XLA Ops:
  0.6 1.0 copy-start
  1.7 0.9 copy-start.2
  2.6 0.9 copy-start.3
  3.5 0.8 copy-start.4
  4.3 0.8 copy-start.5
  5.2 0.7 copy-start.6
  5.9 70.4 %copy-start.1 = (f32[2,128,384]{2,1,0:T(8,128)S(1)}, f32[2,128,384]{2,1,0:T(8,128)}, u32[]{:S(2)}) copy-start(f32[2,128,384]{2,1,0:T(8,128)} %constant.15.clone.iz_hbm) | copy-start | bytes 1179652
  94.2 0.6 copy-start.7

commit v2 on v0

v2 whole, which is shorter than its diff:
```python
import jax
import jax.numpy as jnp
import ml_dtypes
import numpy as np
from jax import lax
from jax.experimental import pallas as pl
from jax.experimental.pallas import tpu as pltpu
from jax.sharding import PartitionSpec as P

F32 = jnp.float32
BF16 = jnp.bfloat16
MESH = pl.DeviceIdType.MESH

SCREEN = 0.002
DIAG = 6.0 + SCREEN
INV_DIAG = 1.0 / DIAG

BX, BY, BZ = 64, 64, 256
CX, CY, CZ = 16, 16, 64
NC = 128
GX, GY, GZ = 8, 8, 2
GROUP = GY * GZ
KZ = NC // GROUP
SENT = 20
ROWS = 24
LOADS = 8
PLANES = BX // LOADS
PARTS = 4
DEEP = BX // PARTS
ORDER = (0, 3, 1, 2)
TOP = 8
PADDED = BY + 16
LOW, MID, HIGH = pl.ds(TOP - 1, BY), pl.ds(TOP, BY), pl.ds(TOP + 1, BY)


def tables():
    def cas(k, n):
        angle = 2.0 * np.pi * ((k * n) % NC) / NC
        return np.cos(angle) + np.sin(angle)

    def pair(t):
        high = t.astype(ml_dtypes.bfloat16)
        low = (t - high.astype(np.float64)).astype(ml_dtypes.bfloat16)
        return np.stack([high, low], axis=-3)

    mode = np.arange(NC)
    z = np.arange(BZ)
    forward_z = np.zeros((GZ, 2 * BZ, NC))
    inverse_z = np.zeros((GZ, NC, 2 * BZ))
    for b in range(GZ):
        cell = CZ * b + z // 4
        here = cas(cell[:, None], mode[None, :])
        down = np.where((z % 4 == 0)[:, None], cas(cell[:, None] - 1, mode[None, :]) - here, 0.0)
        up = np.where((z % 4 == 3)[:, None], cas(cell[:, None] + 1, mode[None, :]) - here, 0.0)
        forward_z[b, :BZ] = here
        forward_z[b, BZ:] = down + up
        inverse_z[b, :, :BZ] = here.T
        inverse_z[b, :, BZ:] = (SCREEN * here - down - up).T
    forward_y = cas(mode[:, None], mode[None, :])
    back_y = np.zeros((GY, ROWS, NC))
    for b in range(GY):
        place = np.concatenate([CY * b + np.arange(CY), [CY * b - 1, CY * b + CY]])
        back_y[b, : CY + 2] = cas(place[:, None], mode[None, :])
    wave = 2.0 - 2.0 * np.cos(2.0 * np.pi * mode / NC)
    wave_y = np.broadcast_to(wave[:, None], (NC, NC)).astype(np.float32)
    wave_z = np.tile(wave.reshape(GROUP, 1, KZ), (1, CX, 1)).reshape(GROUP, NC).astype(np.float32)
    return (
        pair(forward_z), pair(inverse_z), pair(forward_y), pair(back_y.reshape(GY * ROWS, NC)),
        np.ascontiguousarray(wave_y), wave_z,
    )


def split(a):
    high = a.astype(BF16)
    return high, (a - high.astype(F32)).astype(BF16)


def product(a, b):
    return jnp.dot(a, b, preferred_element_type=F32)


def dot_right(a, table):
    high, low = split(a)
    return product(high, table[0]) + (product(high, table[1]) + product(low, table[0]))


def dot_left(table, b):
    high, low = split(b)
    return product(table[0], high) + (product(table[0], low) + product(table[1], high))


def iota(shape, dim):
    return lax.broadcasted_iota(jnp.int32, shape, dim)


def neighbour_sum(ref, p, edges, i):
    lane = iota((BY, 128), 1)
    first, last = lane == 0, lane == 127
    a0, a1 = ref[p, 0, MID, :], ref[p, 1, MID, :]
    low = jnp.concatenate(
        [pltpu.roll(edges, lax.rem(128 - (32 * q + i), 128), 1) for q in range(4)], axis=0
    )
    high = jnp.concatenate([pltpu.roll(edges, 111 - 32 * q - i, 1) for q in range(4)], axis=0)
    up0, up1 = pltpu.roll(a0, 1, 1), pltpu.roll(a1, 1, 1)
    down0, down1 = pltpu.roll(a0, 127, 1), pltpu.roll(a1, 127, 1)
    sums = (
        jnp.where(first, low, up0) + jnp.where(last, down1, down0),
        jnp.where(first, up0, up1) + jnp.where(last, high, down1),
    )
    sums = tuple(
        s + ((ref[p - 1, h, MID, :] + ref[p + 1, h, MID, :]) + (ref[p, h, LOW, :] + ref[p, h, HIGH, :]))
        for h, s in enumerate(sums)
    )
    return (a0, a1), sums


def pack_edges(a0, a1, i, held):
    lane = iota((16, 128), 1)
    for q in range(4):
        rows = slice(16 * q, 16 * (q + 1))
        held = jnp.where(lane == 32 * q + i, pltpu.roll(a1[rows], 32 * q + i + 1, 1), held)
        held = jnp.where(lane == 32 * q + 16 + i, pltpu.roll(a0[rows], 32 * q + 16 + i, 1), held)
    return held


def spread_lanes(a):
    a = jnp.where(iota(a.shape, 1) < KZ, a, 0.0)
    for shift in (8, 16, 32, 64):
        a = a + pltpu.roll(a, shift, 1)
    return a


def kernel(
    rs_hbm, g_hbm, fz_hbm, iz_hbm, fy_hbm, iy_hbm, wy_hbm, wz_hbm,
    up_hbm, new_hbm, norm_ref,
    g, rs, res, w, fz, iz, fy, iy, wy, wz,
    row_y, fold, folded, face_send, face_recv, spec, a_send, a_recv, m_send, m_recv, c_send, c_recv,
    z_send, z_recv, basis, pz, corr, shift, n_send, n_recv, n_held, n_last,
    g_sem, rs_sem, t_sem, row_sem, up_sem, new_sem, own_sem,
    f_ss, f_rs, x_ss, x_rs, y_ss, y_rs, z_ss, z_rs, a_ss, a_rs, m_ss, m_rs, c_ss, c_rs,
    n_ss, n_rs, l_ss, l_rs,
):
    bx, by, bz = lax.axis_index("gx"), lax.axis_index("gy"), lax.axis_index("gz")
    me = bz * GY + by
    up_x, down_x = {"gx": lax.rem(bx + 1, GX)}, {"gx": lax.rem(bx + GX - 1, GX)}
    up_y, down_y = {"gy": lax.rem(by + 1, GY)}, {"gy": lax.rem(by + GY - 1, GY)}

    def of_group(t):
        return {"gy": lax.rem(t, GY), "gz": t // GY}

    def remote(src, dst, send, recv, where):
        return pltpu.make_async_remote_copy(src, dst, send, recv, device_id=where, device_id_type=MESH)

    def others(body):
        def step(d, carry):
            body(lax.rem(me + d, GROUP))
            return carry

        lax.fori_loop(1, GROUP, step, 0)

    barrier = pltpu.get_barrier_semaphore()

    def greet(where):
        pl.semaphore_signal(barrier, inc=1, device_id=where, device_id_type=MESH)

    for d in range(1, GX):
        greet({"gx": lax.rem(bx + d, GX)})
    others(lambda t: greet(of_group(t)))

    halves = [pl.ds(0, 128), pl.ds(128, 128)]
    load_row = [
        pltpu.make_async_copy(g_hbm.at[:, row, halves[h]], row_y.at[side, h], row_sem.at[side, h])
        for side, row in ((0, 0), (1, BY - 1))
        for h in range(2)
    ]
    load_g = [
        [
            pltpu.make_async_copy(
                g_hbm.at[pl.ds(PLANES * c, PLANES), :, halves[h]],
                g.at[pl.ds(PLANES * c + 1, PLANES), h, MID, :],
                g_sem.at[c, h],
            )
            for h in range(2)
        ]
        for c in range(LOADS)
    ]
    load_rs = [
        [
            pltpu.make_async_copy(
                rs_hbm.at[pl.ds(PLANES * c, PLANES), :, halves[h]],
                rs.at[pl.ds(PLANES * c, PLANES), h],
                rs_sem.at[c, h],
            )
            for h in range(2)
        ]
        for c in range(LOADS)
    ]
    load_t = [
        pltpu.make_async_copy(src, dst, t_sem.at[i])
        for i, (src, dst) in enumerate(
            ((fz_hbm.at[bz], fz), (iz_hbm.at[bz], iz), (fy_hbm, fy), (iy_hbm, iy), (wy_hbm, wy), (wz_hbm, wz))
        )
    ]

    def start(copies):
        for copy in copies:
            copy.start()

    def wait(copies):
        for copy in copies:
            copy.wait()

    start(load_g[0])
    start(load_g[LOADS - 1])
    start(load_row)
    start(load_rs[0])
    for c in range(1, LOADS - 1):
        start(load_g[c])
        start(load_rs[c])
    start(load_rs[LOADS - 1])
    start(load_t)

    wait(load_g[0])
    wait(load_g[LOADS - 1])
    wait(load_row)

    def every_fourth(ref, base):
        return [ref[pl.ds(base + a, 16, stride=4), :] for a in range(4)]

    def total_of(four):
        return (four[0] + four[1]) + (four[2] + four[3])

    for h in range(2):
        face_send[0, h] = total_of(every_fourth(g.at[1, h], TOP))
        face_send[1, h] = total_of(every_fourth(g.at[BX, h], TOP))
        face_send[2, h] = total_of(every_fourth(row_y.at[0, h], 0))
        face_send[3, h] = total_of(every_fourth(row_y.at[1, h], 0))
    pl.semaphore_wait(barrier, GX - 1 + GROUP - 1)
    faces = [
        remote(face_send.at[i], face_recv.at[i], f_ss.at[i], f_rs.at[i], where)
        for i, where in enumerate((down_x, up_x, down_y, up_y))
    ]
    start(faces)

    def planes_out(phase, array):
        return {
            0: remote(
                array.at[1, :, MID, :], array.at[BX + 1, :, MID, :],
                x_ss.at[phase, 0], x_rs.at[phase, 0], down_x,
            ),
            PARTS - 1: remote(
                array.at[BX, :, MID, :], array.at[0, :, MID, :], x_ss.at[phase, 1], x_rs.at[phase, 1], up_x
            ),
        }

    def rows_out(phase, array, k):
        part = pl.ds(1 + DEEP * k, DEEP)
        return [
            remote(
                array.at[part, :, pl.ds(TOP, 1), :], array.at[part, :, pl.ds(TOP + BY, 1), :],
                y_ss.at[phase, k, 0], y_rs.at[phase, k, 0], down_y,
            ),
            remote(
                array.at[part, :, pl.ds(TOP + BY - 1, 1), :], array.at[part, :, pl.ds(TOP - 1, 1), :],
                y_ss.at[phase, k, 1], y_rs.at[phase, k, 1], up_y,
            ),
        ]

    def edges_out(phase, k):
        return remote(
            z_send.at[phase, k], z_recv.at[phase, k], z_ss.at[phase, k], z_rs.at[phase, k], {"gz": 1 - bz}
        )

    g_planes = planes_out(0, g)
    start(g_planes.values())

    z_send[0] = jnp.zeros((PARTS, 16, 128), F32)

    def fold_plane(X, has_below=True, has_above=True):
        x = 4 * X + 1
        held = z_send[0, X // 4]
        planes = []
        for j in range(4):
            planes.append((g[x + j, 0, MID, :], g[x + j, 1, MID, :]))
        for h in range(2):
            first, last = planes[0][h], planes[3][h]
            plane = (first + planes[1][h]) + (planes[2][h] + last)
            rest = (rs[x - 1, h] + rs[x, h]) + (rs[x + 1, h] + rs[x + 2, h])
            rest = rest - SCREEN * plane - (first + last)
            if has_below:
                rest = rest + g[x - 1, h, MID, :]
            if has_above:
                rest = rest + g[x + 4, h, MID, :]
            fold[h] = rest
            fold[2 + h] = plane
        rows = iota((CY, 128), 0)
        for h in range(2):
            a = every_fourth(fold.at[2 + h], 0)
            before = jnp.where(rows == 0, 0.0, pltpu.roll(a[3], 1, 0))
            after = jnp.where(rows == CY - 1, 0.0, pltpu.roll(a[0], CY - 1, 0))
            folded[X, :, 128 * h : 128 * (h + 1)] = (
                total_of(every_fourth(fold.at[h], 0)) + (before - a[0]) + (after - a[3])
            )
            folded[X, :, BZ + 128 * h : BZ + 128 * (h + 1)] = total_of(a)
        for j in range(4):
            held = pack_edges(planes[j][0], planes[j][1], 4 * lax.rem(X, 4) + j, held)
        z_send[0, X // 4] = held

    def fold_step(X, carry):
        fold_plane(X)
        return carry

    wait(load_rs[0])
    fold_plane(jnp.int32(0), has_below=False)
    for c in range(1, LOADS - 1):
        wait(load_g[c])
        wait(load_rs[c])
        lax.fori_loop(2 * c - 1, 2 * c + 1, fold_step, 0)
    wait(load_rs[LOADS - 1])
    lax.fori_loop(CX - 3, CX - 1, fold_step, 0)
    fold_plane(jnp.int32(CX - 1), has_above=False)

    for copy in faces:
        copy.wait_recv()
    for h in range(2):
        lanes = slice(128 * h, 128 * (h + 1))
        folded[CX - 1, :, lanes] = folded[CX - 1, :, lanes] + face_recv[0, h]
        folded[0, :, lanes] = folded[0, :, lanes] + face_recv[1, h]
        for X in range(CX):
            folded[X, CY - 1 : CY, lanes] = folded[X, CY - 1 : CY, lanes] + face_recv[2, h, X : X + 1, :]
            folded[X, 0:1, lanes] = folded[X, 0:1, lanes] + face_recv[3, h, X : X + 1, :]

    wait(load_t)
    spec[...] = dot_right(folded[...].reshape(CX * CY, 2 * BZ), fz).reshape(CX, CY, NC)
    for X in range(1, CX):
        spec[X] = pltpu.roll(spec[X], KZ * X, 1)

    group = iota((CY, 128), 1) // KZ

    def message_a(t):
        out = jnp.zeros((CY, 128), F32)
        for X in range(CX):
            out = jnp.where(group == lax.rem(t + X, CX), spec[X], out)
        return out

    def copy_a(t, slot):
        return remote(a_send.at[t], a_recv.at[slot], a_ss.at[t], a_rs.at[slot], of_group(t))

    def send_a(t):
        a_send[t] = message_a(t)
        copy_a(t, me).start()

    others(send_a)
    a_recv[me] = message_a(me)

    g_rows = [copy for k in range(PARTS) for copy in rows_out(0, g, k)]
    g_edges = [edges_out(0, k) for k in range(PARTS)]
    start(g_rows)
    start(g_edges)

    place = iota((NC, 128), 1) // KZ
    wave = SCREEN * 16.0 + wy[...] + wz[pl.ds(me, 1), :]
    r = 1.0 / (1.0 + 0.5 * wave + jnp.sqrt(wave + 0.25 * wave * wave))
    r2 = r * r
    r4 = r2 * r2
    r8 = r4 * r4
    r16 = r8 * r8

    for copy in list(g_planes.values()) + g_rows:
        copy.wait_recv()
    res_planes = planes_out(1, res)
    res_rows = [rows_out(1, res, k) for k in range(PARTS)]
    res_edges = [edges_out(1, k) for k in range(PARTS)]

    def residual_of(k):
        edges = z_recv[0, k]

        def step(i, held):
            x = DEEP * k + i
            a, near = neighbour_sum(g, x + 1, edges, i)
            out = []
            for h in range(2):
                out.append(rs[x, h] - (DIAG * a[h] - near[h]))
                res[x + 1, h, MID, :] = out[h]
            return pack_edges(out[0], out[1], i, held)

        return step

    def by_two(step):
        return lambda i, held: step(2 * i + 1, step(2 * i, held))

    zero = jnp.zeros((16, 128), F32)
    for k in ORDER:
        g_edges[k].wait_recv()
        z_send[1, k] = lax.fori_loop(0, DEEP // 2, by_two(residual_of(k)), zero)
        if k in res_planes:
            res_planes[k].start()
        start(res_rows[k])
        res_edges[k].start()

    others(lambda t: copy_a(t, t).wait_recv())
    lines = (a_recv[0:GY] + a_recv[GY:GROUP]).reshape(NC, 128)
    u = pltpu.roll(dot_left(fy, lines), lax.rem(128 - KZ * me + 128, 128), 1)

    right, left = u, u
    for step, power in ((1, r), (2, r2), (4, r4), (8, r8)):
        right = right + jnp.where(place >= step, power * pltpu.roll(right, KZ * step, 1), 0.0)
        left = left + jnp.where(place < CX - step, power * pltpu.roll(left, 128 - KZ * step, 1), 0.0)
    lane = iota((NC, 128), 1)
    ends = jnp.where(lane < KZ, left, pltpu.roll(right, 2 * KZ, 1))
    slot16 = iota((CX, 128), 1) // (2 * KZ)
    packed = jnp.zeros((CX, 128), F32)
    decay = jnp.zeros((CX, 128), F32)
    for i in range(8):
        part = ends[CX * i : CX * (i + 1)]
        packed = jnp.where(slot16 == i, pltpu.roll(part, 2 * KZ * i, 1) if i else part, packed)
        decay = jnp.where(slot16 == i, r16[CX * i : CX * (i + 1)], decay)
    m_send[...] = packed
    m_recv[0] = packed
    m_copies = [
        remote(m_send, m_recv.at[d], m_ss.at[d], m_rs.at[d], {"gx": lax.rem(bx + d, GX)}) for d in range(1, GX)
    ]
    start(m_copies)

    end_left, end_right = spread_lanes(left), spread_lanes(pltpu.roll(right, KZ, 1))
    from_low, from_high = r, r
    for bit, power in ((1, r), (2, r2), (4, r4), (8, r8)):
        has = (place // bit) % 2 == 1
        from_low = from_low * jnp.where(has, power, 1.0)
        from_high = from_high * jnp.where(has, 1.0, power)
    scale = (0.25 / (NC * NC)) * r / (1.0 - r2)
    local = right + left - u
    decay8 = decay * decay
    decay8 = decay8 * decay8
    decay8 = decay8 * decay8
    wrap = 1.0 / (1.0 - decay8)

    w_planes = planes_out(2, w)
    w_rows = [rows_out(2, w, k) for k in range(PARTS)]
    w_edges = [edges_out(2, k) for k in range(PARTS)]

    def fix_of(k):
        edges = z_recv[1, k]

        def step(i, held):
            x = DEEP * k + i
            a, near = neighbour_sum(res, x + 1, edges, i)
            out = []
            for h in range(2):
                out.append(g[x + 1, h, MID, :] + (a[h] + near[h] * INV_DIAG) * INV_DIAG)
                w[x + 1, h, MID, :] = out[h]
            return pack_edges(out[0], out[1], i, held)

        return step

    for k in ORDER:
        if k in res_planes:
            res_planes[PARTS - 1 - k].wait_recv()
        for copy in res_rows[k] + [res_edges[k]]:
            copy.wait_recv()
        z_send[2, k] = lax.fori_loop(0, DEEP // 2, by_two(fix_of(k)), zero)
        if k in w_planes:
            w_planes[k].start()
        start(w_rows[k])
        w_edges[k].start()

    for copy in m_copies:
        copy.wait_recv()
    is_right = (iota((CX, 128), 1) // KZ) % 2 == 1
    incoming = jnp.zeros((CX, 128), F32)
    for d in range(GX, 0, -1):
        incoming = jnp.where(is_right, m_recv[d % GX], m_recv[(GX - d) % GX]) + decay * incoming
    incoming = incoming * wrap
    unpacked = jnp.concatenate(
        [pltpu.roll(incoming, 128 - 2 * KZ * i, 1) if i else incoming for i in range(8)], axis=0
    )
    in_left, in_right = spread_lanes(unpacked), spread_lanes(pltpu.roll(unpacked, 128 - KZ, 1))
    solved = scale * (local + from_low * in_right + from_high * in_left)
    before = scale * (r * end_left + in_right + r16 * (r * in_left))
    after = scale * (r * end_right + in_left + r16 * (r * in_right))

    lines = dot_left(iy, jnp.concatenate([pltpu.roll(solved, KZ * me, 1), before, after], axis=1))
    diagonal = iota((CY, 128), 0) == iota((CY, 128), 1) // KZ
    for b in range(GY):
        rows = slice(ROWS * b, ROWS * b + CY)
        c_send[b] = lines[ROWS * b : ROWS * (b + 1), :128]
        for side in range(2):
            plane = jnp.where(diagonal, lines[rows, 128 * (side + 1) : 128 * (side + 2)], 0.0)
            c_send[b, CY + 2 + side : CY + 3 + side, :] = jnp.sum(plane, axis=0, keepdims=True)

    sent = pl.ds(0, SENT)

    def copy_c(t, slot):
        return remote(
            c_send.at[lax.rem(t, GY), sent], c_recv.at[slot, sent], c_ss.at[t], c_rs.at[slot], of_group(t)
        )

    others(lambda t: copy_c(t, me).start())
    c_recv[me] = c_send[by]

    def before_of(k):
        edges = z_recv[2, k]

        def step(i, carry):
            x = DEEP * k + i
            a, near = neighbour_sum(w, x + 1, edges, i)
            for h in range(2):
                rs[x, h] = rs[x, h] - (DIAG * a[h] - near[h])
            return carry

        return step

    for k in ORDER:
        if k in w_planes:
            w_planes[PARTS - 1 - k].wait_recv()
        for copy in w_rows[k] + [w_edges[k]]:
            copy.wait_recv()
        lax.fori_loop(0, DEEP // 2, by_two(before_of(k)), 0)

    for copies in (w_rows + [list(w_planes.values())]):
        for copy in copies:
            copy.wait_send()

    others(lambda t: copy_c(t, t).wait_recv())

    group = iota((ROWS, 128), 1) // KZ

    def gather(X):
        out = jnp.zeros((ROWS, 128), F32)
        for t in range(GROUP):
            out = jnp.where(group == lax.rem(X + t, CX), c_recv[t], out)
        basis[X + 1] = pltpu.roll(out, lax.rem(128 - KZ * X + 128, 128), 1)

    def gather_step(i, carry):
        gather(2 * i)
        gather(2 * i + 1)
        return carry

    lax.fori_loop(0, CX // 2, gather_step, 0)
    spot = iota((CY, 128), 1) // KZ
    for side, X in ((0, 0), (1, CX + 1)):
        out = jnp.zeros((CY, 128), F32)
        for t in range(GROUP):
            line = jnp.where(diagonal, c_recv[t, CY + 2 + side : CY + 3 + side, :], 0.0)
            for move in (8, 16, 32, 64):
                line = line + pltpu.roll(line, move, 1)
            out = jnp.where(spot == t, line, out)
        basis[X, 0:CY, :] = out
        basis[X, CY:, :] = jnp.zeros((ROWS - CY, 128), F32)

    pz[...] = dot_right(basis[...].reshape((CX + 2) * ROWS, NC), iz).reshape(CX + 2, ROWS, 2 * BZ)

    def put(ref, X, h, four):
        for a in range(4):
            ref[X, h, pl.ds(a, CY, stride=4), :] = four[a]

    for X in (0, CX + 1):
        for h in range(2):
            put(corr, X, h, [pz[X, 0:CY, 128 * h : 128 * (h + 1)]] * 4)

    def prolong(X, carry):
        row = iota((CY, 128), 0)
        for h in range(2):
            lanes = slice(128 * h, 128 * (h + 1))
            here = pz[X, 0:CY, lanes]
            base = pz[X, 0:CY, BZ + 128 * h : BZ + 128 * (h + 1)]
            below = jnp.where(row == 0, pz[X, CY : CY + 1, lanes], pltpu.roll(here, 1, 0))
            above = jnp.where(row == CY - 1, pz[X, CY + 1 : CY + 2, lanes], pltpu.roll(here, CY - 1, 0))
            put(corr, X, h, [here] * 4)
            put(shift, X - 1, h, [base + (here - below), base, base, base + (here - above)])
        return carry

    lax.fori_loop(1, CX + 1, prolong, 0)

    def finish(X, total):
        for h in range(2):
            here = corr[X + 1, h]
            within = shift[X, h]
            low = here - corr[X, h]
            high = here - corr[X + 2, h]
            for j in range(4):
                x = 4 * X + j
                w[x + 1, h, MID, :] = w[x + 1, h, MID, :] + here
                out = rs[x, h] - within
                if j == 0:
                    out = out - low
                if j == 3:
                    out = out - high
                rs[x, h] = out
                total = total + (out * out).reshape(8, 8, 128).sum(axis=0)
        return total

    total = jnp.zeros((8, 128), F32)
    stores = []
    for c in range(LOADS):
        total = lax.fori_loop(2 * c, 2 * c + 2, finish, total)
        part, shifted = pl.ds(PLANES * c, PLANES), pl.ds(PLANES * c + 1, PLANES)
        now = []
        for h in range(2):
            now.append(
                pltpu.make_async_copy(w.at[shifted, h, MID, :], up_hbm.at[part, :, halves[h]], up_sem.at[c, h])
            )
            now.append(pltpu.make_async_copy(rs.at[part, h], new_hbm.at[part, :, halves[h]], new_sem.at[c, h]))
        start(now)
        stores += now

    n_send[...] = total

    def copy_n(t, slot):
        return remote(n_send, n_recv.at[slot], n_ss.at[t], n_rs.at[slot], of_group(t))

    others(lambda t: copy_n(t, me).start())
    n_recv[me] = total
    others(lambda t: copy_n(t, t).wait_recv())
    total = n_recv[0]
    for t in range(1, GROUP):
        total = total + n_recv[t]
    n_held[...] = total

    def copy_l(d):
        to, slot = lax.rem(bx + d, GX), lax.rem(bx + GX - d, GX)
        return (
            remote(n_held, n_last.at[bx], l_ss.at[d], l_rs.at[bx], {"gx": to}),
            remote(n_held, n_last.at[slot], l_ss.at[d], l_rs.at[slot], {"gx": to}),
        )

    line = [copy_l(d) for d in range(1, GX)]
    for out, _ in line:
        out.start()
    n_last[bx] = total
    for _, back in line:
        back.wait_recv()
    total = n_last[0]
    for b in range(1, GX):
        total = total + n_last[b]
    norm_ref[...] = jnp.sqrt(jnp.full((8, 128), jnp.sum(total), F32))

    for copy in faces + list(g_planes.values()) + g_rows + g_edges + list(res_planes.values()) + res_edges:
        copy.wait_send()
    for copies in res_rows:
        for copy in copies:
            copy.wait_send()
    for copy in w_edges + m_copies:
        copy.wait_send()

    def all_sent(t):
        copy_a(t, t).wait_send()
        copy_c(t, t).wait_send()
        copy_n(t, t).wait_send()

    others(all_sent)
    for out, _ in line:
        out.wait_send()
    wait(stores)


ANY = pl.BlockSpec(memory_space=pl.ANY)
HBM = pl.BlockSpec(memory_space=pltpu.HBM)
IN_VMEM = pl.BlockSpec(memory_space=pltpu.VMEM)
DMA = pltpu.SemaphoreType.DMA
VMEM = pltpu.VMEM


def per_device(right_side, guess):
    shape = jax.ShapeDtypeStruct
    block = (BX, BY, BZ)
    padded = (BX + 2, 2, PADDED, 128)
    updated, new_residual, norm = pl.pallas_call(
        kernel,
        out_shape=(shape(block, F32), shape(block, F32), shape((8, 128), F32)),
        in_specs=[HBM] * 8,
        out_specs=(ANY, ANY, IN_VMEM),
        scratch_shapes=[
            VMEM(padded, F32), VMEM((BX, 2, BY, 128), F32), VMEM(padded, F32), VMEM(padded, F32),
            VMEM((2, 2 * BZ, NC), BF16), VMEM((2, NC, 2 * BZ), BF16), VMEM((2, NC, NC), BF16),
            VMEM((2, GY * ROWS, NC), BF16), VMEM((NC, NC), F32), VMEM((GROUP, NC), F32),
            VMEM((2, 2, BX, 128), F32), VMEM((4, BY, 128), F32), VMEM((CX, CY, 2 * BZ), F32),
            VMEM((4, 2, CX, 128), F32), VMEM((4, 2, CX, 128), F32),
            VMEM((CX, CY, 128), F32), VMEM((GROUP, CY, 128), F32), VMEM((GROUP, CY, 128), F32),
            VMEM((CX, 128), F32), VMEM((GX, CX, 128), F32),
            VMEM((GY, ROWS, 128), F32), VMEM((GROUP, ROWS, 128), F32),
            VMEM((3, PARTS, 16, 128), F32), VMEM((3, PARTS, 16, 128), F32),
            VMEM((CX + 2, ROWS, 128), F32), VMEM((CX + 2, ROWS, 2 * BZ), F32),
            VMEM((CX + 2, 2, BY, 128), F32), VMEM((CX, 2, BY, 128), F32),
            VMEM((8, 128), F32), VMEM((GROUP, 8, 128), F32), VMEM((8, 128), F32), VMEM((GX, 8, 128), F32),
            DMA((LOADS, 2)), DMA((LOADS, 2)), DMA((6,)), DMA((2, 2)), DMA((LOADS, 2)), DMA((LOADS, 2)), DMA,
            DMA((4,)), DMA((4,)), DMA((3, 2)), DMA((3, 2)), DMA((3, PARTS, 2)), DMA((3, PARTS, 2)),
            DMA((3, PARTS)), DMA((3, PARTS)), DMA((GROUP,)), DMA((GROUP,)), DMA((GX,)), DMA((GX,)),
            DMA((GROUP,)), DMA((GROUP,)), DMA((GROUP,)), DMA((GROUP,)), DMA((GX,)), DMA((GX,)),
        ],
        compiler_params=pltpu.CompilerParams(
            collective_id=0, has_side_effects=True, vmem_limit_bytes=48 * 1024 * 1024
        ),
        name="schwarz",
    )(right_side, guess, *[jnp.asarray(t) for t in tables()])
    return updated, new_residual, norm[0, 0]


def solution(mesh):
    spec = P("gx", "gy", "gz")
    return jax.shard_map(
        per_device, mesh=mesh, in_specs=(spec, spec), out_specs=(spec, spec, P()), check_vma=False
    )
```

time: 260 us -> 71.4 us (0.27)
  other arithmetic: 75.5 us -> 0 us
  Pallas kernels: 0 us -> 58.7 us
  starting transfers between devices: 55.2 us -> 0 us
  local copies, waits for them, and re-layouts: 63.3 us -> 11.6 us
  blocking collectives: 38.6 us -> 0 us
  waiting for transfers between devices: 19.2 us -> 0 us
  matrix products: 3.43 us -> 0 us
    pallas_call x0 -> x1, Pallas kernels: none -> 58.7 us  [per_device(): pl.pallas_call(kernel, out_shape=(shape(block, F32), shape(block, F32), s...]
    psum x5 -> x0, blocking collectives: 38.6 us -> none  [over_axes(): return functools.reduce(lax.psum, axes, shard)]
    ppermute x18 -> x0, starting transfers between devices: 29.5 us -> none  [the longest x9 18.2 us: with_halo(): lax.ppermute(leading, axis, [(b, a) for a, b in up])]
    reduce_sum x2 -> x0, other arithmetic: 28.2 us -> none  [the longest x1 24.7 us: per_device(): total = over_axes(jnp.sum(new_residual * new_residual), GX_GY_GZ)]
    all_to_all x6 -> x0, starting transfers between devices: 25.7 us -> none  [the longest x1 6.37 us: per_device(): lax.all_to_all(spectra, GY, split_axis=1, concat_axis=2, tiled=True)]
    add x3 -> x0, other arithmetic: 23 us -> none  [the longest x1 22.4 us: per_device(): updated = guess + local_fix + prolonged]
    slice x13 -> x1, local copies, waits for them, and re-layouts: 21.9 us -> 0.51 us  [per_device(): return (updated, new_residual, norm[0, 0])]
    div x4 -> x0, other arithmetic: 18.8 us -> none  [the longest x1 18.6 us: per_device(): first_sweep = residual_now / diag_value]
  transfers between devices with their start and end apart: 24 -> 0, of which waited for: 6 -> 0; matrix products, arithmetic and copies ran while one was open for 20% -> 0% of each run, Pallas kernels for 0% -> 0%
where the time goes in v2:
time: 71.4 us; the launch traced here: 71 us
  Pallas kernels  58.7 us (82%)
  local copies, waits for them, and re-layouts  11.6 us (16%)
    pallas_call x1, Pallas kernels, per_device(): pl.pallas_call(kernel, out_shape=(shape(block, F32), shape(block, F32), s...  58.7 us
    unnamed x16, local copies, waits for them, and re-layouts  11.1 us

profile of v2, /device:TPU:1, one launch (start us, length us, event | category | flops | bytes accessed | tf_op | source)
XLA Modules:
  0.0 71.0 jit_solution(5615471277784494757)
XLA Ops:
  0.6 0.0 copy-start
  0.6 1.0 %copy-done = bf16[2,2,128,512]{3,2,1,0:T(8,128)(2,1)S(1)} copy-done((bf16[2,2,128,512]{3,2,1,0:T(8,128)(2,1)S(1)}, bf16[2,2,128,512]{3,2,1,0:T(8,128)(2,1)}, u32[]{:S(2)}) %copy-start) | copy-done | bytes 524312
  1.7 0.0 copy-start.1
  1.7 1.0 %copy-done.1 = bf16[2,2,512,128]{3,2,1,0:T(8,128)(2,1)S(1)} copy-done((bf16[2,2,512,128]{3,2,1,0:T(8,128)(2,1)S(1)}, bf16[2,2,512,128]{3,2,1,0:T(8,128)(2,1)}, u32[]{:S(2)}) %copy-start.1) | copy-done | bytes 524312
  2.7 0.0 copy-start.2
  2.7 0.9 %copy-done.2 = bf16[2,192,128]{2,1,0:T(8,128)(2,1)S(1)} copy-done((bf16[2,192,128]{2,1,0:T(8,128)(2,1)S(1)}, bf16[2,192,128]{2,1,0:T(8,128)(2,1)}, u32[]{:S(2)}) %copy-start.2) | copy-done | bytes 98328
  3.6 0.0 copy-start.3
  3.6 0.8 %copy-done.3 = f32[128,128]{1,0:T(8,128)S(1)} copy-done((f32[128,128]{1,0:T(8,128)S(1)}, f32[128,128]{1,0:T(8,128)}, u32[]{:S(2)}) %copy-start.3) | copy-done | bytes 65560
  4.5 0.0 copy-start.4
  4.5 0.8 %copy-done.4 = bf16[2,128,128]{2,1,0:T(8,128)(2,1)S(1)} copy-done((bf16[2,128,128]{2,1,0:T(8,128)(2,1)S(1)}, bf16[2,128,128]{2,1,0:T(8,128)(2,1)}, u32[]{:S(2)}) %copy-start.4) | copy-done | bytes 65560
  5.3 0.0 copy-start.5
  5.3 0.7 copy-done.5
  6.0 58.7 %schwarz.1 = (f32[64,64,256]{2,1,0:T(8,128)S(1)}, f32[64,64,256]{2,1,0:T(8,128)}, f32[8,128]{1,0:T(8,128)S(1)}) custom-call(f32[64,64,256]{2,1,0:T(8,128)} %rs_hbm.1, f32[64,64,256]{2,1,0:T(8,128)} %g_hbm.1, bf16[2,2,512,128]{3,2,1,0:T(8,128)(2,1)S(1)} %copy-done.1, bf16[2,2,128,512]{3,2,1,0:T(8,128)(2,1)S(1)} %copy-done, ...), custom_call_target="tpu_custom_call" | custom-call | tf_op jit(solution)/shard_map/schwarz/pallas_call | solution.py:668
  64.7 0.5 slice.3
  65.2 0.0 copy-start.6
  65.2 2.1 %copy.13 = f32[64,64,256]{2,1,0:T(8,128)} copy(f32[64,64,256]{2,1,0:T(8,128)S(1)} %get-tuple-element.12) | data formatting | bytes 8388608
  67.4 1.6 %copy-done.6 = f32[64,64,256]{2,1,0:T(8,128)S(1)} copy-done((f32[64,64,256]{2,1,0:T(8,128)S(1)}, f32[64,64,256]{2,1,0:T(8,128)}, u32[]{:S(2)}) %copy-start.6) | copy-done | bytes 4194328
  68.9 2.0 %copy.14 = f32[64,64,256]{2,1,0:T(8,128)} copy(f32[64,64,256]{2,1,0:T(8,128)S(1)} %copy-done.6) | data formatting | bytes 8388608
Async XLA Ops:
  0.6 1.0 %copy-start = (bf16[2,2,128,512]{3,2,1,0:T(8,128)(2,1)S(1)}, bf16[2,2,128,512]{3,2,1,0:T(8,128)(2,1)}, u32[]{:S(2)}) copy-start(bf16[2,2,128,512]{3,2,1,0:T(8,128)(2,1)} %constant.13.clone.iz_hbm) | copy-start | bytes 1572868
  1.7 1.0 %copy-start.1 = (bf16[2,2,512,128]{3,2,1,0:T(8,128)(2,1)S(1)}, bf16[2,2,512,128]{3,2,1,0:T(8,128)(2,1)}, u32[]{:S(2)}) copy-start(bf16[2,2,512,128]{3,2,1,0:T(8,128)(2,1)} %constant.12.clone.fz_hbm) | copy-start | bytes 1572868
  2.7 0.9 %copy-start.2 = (bf16[2,192,128]{2,1,0:T(8,128)(2,1)S(1)}, bf16[2,192,128]{2,1,0:T(8,128)(2,1)}, u32[]{:S(2)}) copy-start(bf16[2,192,128]{2,1,0:T(8,128)(2,1)} %constant.15.clone.iy_hbm) | copy-start | bytes 294916
  3.6 0.8 %copy-start.3 = (f32[128,128]{1,0:T(8,128)S(1)}, f32[128,128]{1,0:T(8,128)}, u32[]{:S(2)}) copy-start(f32[128,128]{1,0:T(8,128)} %constant.16.clone.wy_hbm) | copy-start | bytes 196612
  4.5 0.8 %copy-start.4 = (bf16[2,128,128]{2,1,0:T(8,128)(2,1)S(1)}, bf16[2,128,128]{2,1,0:T(8,128)(2,1)}, u32[]{:S(2)}) copy-start(bf16[2,128,128]{2,1,0:T(8,128)(2,1)} %constant.14.clone.fy_hbm) | copy-start | bytes 196612
  5.3 0.7 copy-start.5
  65.2 3.7 %copy-start.6 = (f32[64,64,256]{2,1,0:T(8,128)S(1)}, f32[64,64,256]{2,1,0:T(8,128)}, u32[]{:S(2)}) copy-start(f32[64,64,256]{2,1,0:T(8,128)} %get-tuple-element.13) | copy-start | bytes 12582916

commit v3 on v2

v3 whole, which is shorter than its diff:
```python
import math

import jax
import jax.numpy as jnp
from jax import lax
from jax.experimental import pallas as pl
from jax.experimental.pallas import tpu as pltpu
from jax.sharding import PartitionSpec as P

F32 = jnp.float32
BF16 = jnp.bfloat16
MESH = pl.DeviceIdType.MESH

SCREEN = 0.002
DIAG = 6.0 + SCREEN
INV_DIAG = 1.0 / DIAG

BX, BY, BZ = 64, 64, 256
CX, CY, CZ = 16, 16, 64
NC = 128
GX, GY, GZ = 8, 8, 2
GROUP = GY * GZ
KZ = NC // GROUP
ROWS = 24
LOADS = 8
PLANES = BX // LOADS
PARTS = 4
DEEP = BX // PARTS
TOGETHER = 4
ORDER = (0, 3, 1, 2)
TOP = 8
PADDED = BY + 16
LOW, MID, HIGH = pl.ds(TOP - 1, BY), pl.ds(TOP, BY), pl.ds(TOP + 1, BY)


def sine(t):
    a = t.astype(F32) * (math.pi / 128.0)
    b = a * a
    p = -1.0 / 39916800.0
    for c in (1.0 / 362880.0, -1.0 / 5040.0, 1.0 / 120.0, -1.0 / 6.0, 1.0):
        p = p * b + c
    return a * p


def cas(product_of_indices):
    half = sine(jnp.abs(((product_of_indices - 16) & (NC - 1)) - 64))
    return math.sqrt(2.0) * (2.0 * half * half - 1.0)


def wave_of(k):
    half = sine(64 - jnp.abs(k - 64))
    return 4.0 * half * half


def split(a):
    high = a.astype(BF16)
    return high, (a - high.astype(F32)).astype(BF16)


def product(a, b):
    return jnp.dot(a, b, preferred_element_type=F32)


def dot_right(a, table):
    high, low = split(a)
    return product(high, table[0]) + (product(high, table[1]) + product(low, table[0]))


def dot_left(table, b):
    high, low = split(b)
    return product(table[0], high) + (product(table[0], low) + product(table[1], high))


def iota(shape, dim):
    return lax.broadcasted_iota(jnp.int32, shape, dim)


def mod(a, b):
    return a % b if isinstance(a, int) else lax.rem(a, b)


def neighbour_sum(ref, p, edges, i):
    lane = iota((BY, 128), 1)
    first, last = lane == 0, lane == 127
    a0, a1 = ref[p, 0, MID, :], ref[p, 1, MID, :]
    edge = jnp.concatenate([pltpu.roll(edges, 127 - 32 * q - 2 * i, 1) for q in range(4)], axis=0)
    up0, up1 = pltpu.roll(a0, 1, 1), pltpu.roll(a1, 1, 1)
    down0, down1 = pltpu.roll(a0, 127, 1), pltpu.roll(a1, 127, 1)
    sums = (
        jnp.where(first, edge, up0) + jnp.where(last, down1, down0),
        jnp.where(first, up0, up1) + jnp.where(last, edge, down1),
    )
    sums = tuple(
        s + ((ref[p - 1, h, MID, :] + ref[p + 1, h, MID, :]) + (ref[p, h, LOW, :] + ref[p, h, HIGH, :]))
        for h, s in enumerate(sums)
    )
    return (a0, a1), sums


def pack_edges(planes, i, held):
    lane = iota((16, 128), 1)
    end = lane == 127
    for j in range(len(planes) + 1):
        for q in range(4):
            rows = slice(16 * q, 16 * (q + 1))
            place = 32 * q + 2 * (i + j)
            if j == 0:
                value, mask = planes[0][0][rows], lane == place
            elif j == len(planes):
                value, mask = planes[-1][1][rows], lane == place - 1
            else:
                value = jnp.where(end, planes[j - 1][1][rows], planes[j][0][rows])
                mask = (lane == place) | (lane == place - 1)
            held = jnp.where(mask, pltpu.roll(value, mod(place, 128), 1), held)
    return held


def spread_lanes(a):
    a = jnp.where(iota(a.shape, 1) < KZ, a, 0.0)
    for shift in (8, 16, 32, 64):
        a = a + pltpu.roll(a, shift, 1)
    return a


def kernel(
    rs_hbm, g_hbm,
    up_ref, new_ref, norm_ref,
    g, rs, res, w, fz, iz, fy, iy, py,
    fold, folded, extra, spec, a_send, a_recv, m_send, m_recv, v_send, v_recv, c_send, c_recv,
    z_send, z_recv, basis, pz, corr, shift, n_send, n_recv, n_held, n_last,
    g_sem, rs_sem, v_ss, v_rs, x_ss, x_rs, y_ss, y_rs, z_ss, z_rs, a_ss, a_rs, m_ss, m_rs, c_ss, c_rs,
    n_ss, n_rs, l_ss, l_rs,
):
    bx, by, bz = lax.axis_index("gx"), lax.axis_index("gy"), lax.axis_index("gz")
    me = bz * GY + by
    up_x, down_x = {"gx": lax.rem(bx + 1, GX)}, {"gx": lax.rem(bx + GX - 1, GX)}
    up_y, down_y = {"gy": lax.rem(by + 1, GY)}, {"gy": lax.rem(by + GY - 1, GY)}

    def of_group(t):
        return {"gy": lax.rem(t, GY), "gz": t // GY}

    def remote(src, dst, send, recv, where):
        return pltpu.make_async_remote_copy(src, dst, send, recv, device_id=where, device_id_type=MESH)

    def others(body):
        def step(d, carry):
            body(lax.rem(me + d, GROUP))
            return carry

        lax.fori_loop(1, GROUP, step, 0)

    barrier = pltpu.get_barrier_semaphore()

    def greet(where):
        pl.semaphore_signal(barrier, inc=1, device_id=where, device_id_type=MESH)

    for d in range(1, GX):
        greet({"gx": lax.rem(bx + d, GX)})
    others(lambda t: greet(of_group(t)))

    halves = [pl.ds(0, 128), pl.ds(128, 128)]
    load_g = [
        [
            pltpu.make_async_copy(
                g_hbm.at[pl.ds(PLANES * c, PLANES), :, halves[h]],
                g.at[pl.ds(PLANES * c + 1, PLANES), h, MID, :],
                g_sem.at[c, h],
            )
            for h in range(2)
        ]
        for c in range(LOADS)
    ]
    load_rs = [
        [
            pltpu.make_async_copy(
                rs_hbm.at[pl.ds(PLANES * c, PLANES), :, halves[h]],
                rs.at[pl.ds(PLANES * c, PLANES), h],
                rs_sem.at[c, h],
            )
            for h in range(2)
        ]
        for c in range(LOADS)
    ]
    def start(copies):
        for copy in copies:
            copy.start()

    def wait(copies):
        for copy in copies:
            copy.wait()

    start(load_g[0])
    start(load_g[LOADS - 1])
    start(load_rs[0])
    for c in range(1, LOADS - 1):
        start(load_g[c])
        start(load_rs[c])
    start(load_rs[LOADS - 1])

    def keep(ref, rows, lanes, value):
        high, low = split(value)
        ref[0, rows, lanes] = high
        ref[1, rows, lanes] = low

    def beside(z):
        cell = CZ * bz + z // 4
        return cell, cell + jnp.where(z % 4 == 3, 1, 0) - jnp.where(z % 4 == 0, 1, 0)

    whole = slice(None)
    for part in range(4):
        cell, near = beside(iota((64, NC), 0) + 64 * part)
        mode = iota((64, NC), 1)
        here = cas(cell * mode)
        keep(fz, slice(64 * part, 64 * (part + 1)), whole, here)
        keep(fz, slice(BZ + 64 * part, BZ + 64 * (part + 1)), whole, cas(near * mode) - here)
    for part in range(2):
        cell, near = beside(iota((NC, 128), 1) + 128 * part)
        mode = iota((NC, 128), 0)
        here = cas(cell * mode)
        keep(iz, whole, slice(128 * part, 128 * (part + 1)), here)
        keep(iz, whole, slice(BZ + 128 * part, BZ + 128 * (part + 1)), SCREEN * here - (cas(near * mode) - here))

    keep(py, whole, whole, cas(iota((NC, NC), 0) * iota((NC, NC), 1)))

    def place_of(index):
        b = (index * 2731) >> 16
        Y = index - ROWS * b
        place = CY * b + jnp.where(Y == CY, -1, jnp.where(Y == CY + 1, CY, Y))
        return place, Y < CY + 2

    place, used = place_of(iota((NC, GY * ROWS), 1))
    keep(fy, whole, whole, jnp.where(used, cas(place * iota((NC, GY * ROWS), 0)), 0.0))
    place, used = place_of(iota((GY * ROWS, NC), 0))
    keep(iy, whole, whole, jnp.where(used, cas(place * iota((GY * ROWS, NC), 1)), 0.0))

    wait(load_g[0])
    wait(load_g[LOADS - 1])

    def every_fourth(ref, base):
        return [ref[pl.ds(base + a, 16, stride=4), :] for a in range(4)]

    def total_of(four):
        return (four[0] + four[1]) + (four[2] + four[3])

    for h in range(2):
        extra[h, 2 * CX : 3 * CX, :] = total_of(every_fourth(g.at[1, h], TOP))
        extra[h, 3 * CX :, :] = total_of(every_fourth(g.at[BX, h], TOP))

    def planes_out(phase, array):
        return {
            0: remote(
                array.at[1, :, MID, :], array.at[BX + 1, :, MID, :],
                x_ss.at[phase, 0], x_rs.at[phase, 0], down_x,
            ),
            PARTS - 1: remote(
                array.at[BX, :, MID, :], array.at[0, :, MID, :], x_ss.at[phase, 1], x_rs.at[phase, 1], up_x
            ),
        }

    def rows_out(phase, array, k):
        part = pl.ds(1 + DEEP * k, DEEP)
        return [
            remote(
                array.at[part, :, pl.ds(TOP, 1), :], array.at[part, :, pl.ds(TOP + BY, 1), :],
                y_ss.at[phase, k, 0], y_rs.at[phase, k, 0], down_y,
            ),
            remote(
                array.at[part, :, pl.ds(TOP + BY - 1, 1), :], array.at[part, :, pl.ds(TOP - 1, 1), :],
                y_ss.at[phase, k, 1], y_rs.at[phase, k, 1], up_y,
            ),
        ]

    def edges_out(phase, k):
        return remote(
            z_send.at[phase, k], z_recv.at[phase, k], z_ss.at[phase, k], z_rs.at[phase, k], {"gz": 1 - bz}
        )

    z_send[0] = jnp.zeros((PARTS, 16, 128), F32)

    def fold_plane(X, has_below=True, has_above=True):
        x = 4 * X + 1
        planes = []
        for j in range(4):
            planes.append((g[x + j, 0, MID, :], g[x + j, 1, MID, :]))
        for h in range(2):
            first, last = planes[0][h], planes[3][h]
            plane = (first + planes[1][h]) + (planes[2][h] + last)
            rest = (rs[x - 1, h] + rs[x, h]) + (rs[x + 1, h] + rs[x + 2, h])
            rest = rest - SCREEN * plane - (first + last)
            if has_below:
                rest = rest + g[x - 1, h, MID, :]
            if has_above:
                rest = rest + g[x + 4, h, MID, :]
            fold[h] = rest
            fold[2 + h] = plane
        rows = iota((CY, 128), 0)
        for h in range(2):
            a = every_fourth(fold.at[2 + h], 0)
            before = jnp.where(rows == 0, 0.0, pltpu.roll(a[3], 1, 0))
            after = jnp.where(rows == CY - 1, 0.0, pltpu.roll(a[0], CY - 1, 0))
            folded[X, :, 128 * h : 128 * (h + 1)] = (
                total_of(every_fourth(fold.at[h], 0)) + (before - a[0]) + (after - a[3])
            )
            folded[X, :, BZ + 128 * h : BZ + 128 * (h + 1)] = total_of(a)
            extra[h, pl.ds(X, 1), :] = fold[2 + h, 0:1, :]
            extra[h, pl.ds(CX + X, 1), :] = fold[2 + h, BY - 1 : BY, :]
        z_send[0, X // 4] = pack_edges(planes, 4 * mod(X, 4), z_send[0, X // 4])

    def fold_step(X, carry):
        fold_plane(X)
        return carry

    g_planes = planes_out(0, g)
    g_rows = [rows_out(0, g, k) for k in range(PARTS)]
    g_edges = [edges_out(0, k) for k in range(PARTS)]

    def send_part(k):
        start(g_rows[k])
        g_edges[k].start()

    wait(load_rs[0])
    fold_plane(0, has_below=False)
    for c in range(1, LOADS - 1):
        wait(load_g[c])
        wait(load_rs[c])
        lax.fori_loop(2 * c - 1, 2 * c + 1, fold_step, 0)
        if c == 4:
            pl.semaphore_wait(barrier, GX - 1 + GROUP - 1)
            start(g_planes.values())
            send_part(0)
            send_part(1)
    send_part(2)
    wait(load_rs[LOADS - 1])
    lax.fori_loop(CX - 3, CX - 1, fold_step, 0)
    fold_plane(CX - 1, has_above=False)
    send_part(3)

    spec[:, 0:CY, :] = dot_right(folded[...].reshape(CX * CY, 2 * BZ), fz).reshape(CX, CY, NC)
    more = dot_right(jnp.concatenate([extra[0], extra[1]], axis=1), fz.at[:, 0:BZ])
    for X in range(CX):
        spec[X, CY : CY + 1, :] = more[X : X + 1]
        spec[X, CY + 1 : CY + 2, :] = more[CX + X : CX + X + 1]
        if X:
            spec[X, 0 : CY + 2, :] = pltpu.roll(spec[X], KZ * X, 1)[0 : CY + 2]
    row = iota((CY, 128), 0)
    group = iota((CY, 128), 1) // KZ
    sides = []
    for side in range(2):
        plane = more[(2 + side) * CX : (3 + side) * CX]
        for bit in (1, 2, 4, 8):
            plane = jnp.where((row // bit) % 2 == 1, pltpu.roll(plane, KZ * bit, 1), plane)
        sides.append(plane)

    wide = iota((ROWS, 128), 1) // KZ

    def message_a(t, ref, slot):
        out = jnp.zeros((ROWS, 128), F32)
        for X in range(CX):
            out = jnp.where(wide == lax.rem(t + X, CX), spec[X], out)
        ref[slot] = out
        turn = (row + t) % CX
        for side in range(2):
            line = jnp.sum(jnp.where(group == turn, sides[side], 0.0), axis=0, keepdims=True)
            ref[slot, CY + 2 + side : CY + 3 + side, :] = line

    def copy_a(t, slot):
        return remote(a_send.at[t], a_recv.at[slot], a_ss.at[t], a_rs.at[slot], of_group(t))

    def send_a(t):
        message_a(t, a_send, t)
        copy_a(t, me).start()

    others(send_a)
    message_a(me, a_recv, me)

    place = iota((NC, 128), 1) // KZ
    wave = SCREEN * 16.0 + wave_of(iota((NC, 128), 0)) + wave_of(KZ * me + iota((NC, 128), 1) % KZ)
    r = 1.0 / (1.0 + 0.5 * wave + jnp.sqrt(wave + 0.25 * wave * wave))
    r2 = r * r
    r4 = r2 * r2
    r8 = r4 * r4
    r16 = r8 * r8
    inverse = 1.0 / r
    from_low, from_high = r, r
    for bit, power in ((1, r), (2, r2), (4, r4), (8, r8)):
        has = (place // bit) % 2 == 1
        from_low = from_low * jnp.where(has, power, 1.0)
        from_high = from_high * jnp.where(has, 1.0, power)

    for copy in g_planes.values():
        copy.wait_recv()
    res_planes = planes_out(1, res)
    res_rows = [rows_out(1, res, k) for k in range(PARTS)]
    res_edges = [edges_out(1, k) for k in range(PARTS)]

    def residual_of(k):
        edges = z_recv[0, k]

        def step(n, held):
            planes = []
            for j in range(TOGETHER):
                i = TOGETHER * n + j
                x = DEEP * k + i
                a, near = neighbour_sum(g, x + 1, edges, i)
                planes.append([rs[x, h] - (DIAG * a[h] - near[h]) for h in range(2)])
                for h in range(2):
                    res[x + 1, h, MID, :] = planes[j][h]
            return pack_edges(planes, TOGETHER * n, held)

        return step

    zero = jnp.zeros((16, 128), F32)
    for k in ORDER:
        for copy in g_rows[k] + [g_edges[k]]:
            copy.wait_recv()
        z_send[1, k] = lax.fori_loop(0, DEEP // TOGETHER, residual_of(k), zero)
        if k in res_planes:
            res_planes[k].start()
        start(res_rows[k])
        res_edges[k].start()

    others(lambda t: copy_a(t, t).wait_recv())
    lines = a_recv[0:GY] + a_recv[GY:GROUP]
    turn = (row + me) % CX
    beyond = [
        jnp.concatenate(
            [jnp.where(group == turn, lines[b, CY + 2 + side : CY + 3 + side], 0.0) for b in range(GY)], axis=0
        )
        for side in range(2)
    ]
    clean = jnp.where(iota((GY, ROWS, 128), 1) < CY + 2, lines, 0.0).reshape(GY * ROWS, 128)
    u = pltpu.roll(dot_left(fy, clean), lax.rem(128 - KZ * me + 128, 128), 1)
    beyond = dot_left(py, jnp.concatenate(beyond, axis=1))
    out_low, out_high = beyond[:, :128], beyond[:, 128:]
    for move in (8, 16, 32, 64):
        out_low = out_low + pltpu.roll(out_low, move, 1)
        out_high = out_high + pltpu.roll(out_high, move, 1)

    right, left = u, u
    for step, power in ((1, r), (2, r2), (4, r4), (8, r8)):
        right = right + jnp.where(place >= step, power * pltpu.roll(right, KZ * step, 1), 0.0)
        left = left + jnp.where(place < CX - step, power * pltpu.roll(left, 128 - KZ * step, 1), 0.0)
    right = right + from_low * out_low
    left = left + from_high * out_high
    lane = iota((NC, 128), 1)
    outside = jnp.where(lane < KZ, out_low, out_high)
    ends = jnp.where(lane < KZ, left, pltpu.roll(right, 2 * KZ, 1)) + inverse * outside
    slot16 = iota((CX, 128), 1) // (2 * KZ)
    packed = jnp.zeros((CX, 128), F32)
    decay = jnp.zeros((CX, 128), F32)
    packed_out = jnp.zeros((CX, 128), F32)
    for i in range(8):
        part = ends[CX * i : CX * (i + 1)]
        packed = jnp.where(slot16 == i, pltpu.roll(part, 2 * KZ * i, 1) if i else part, packed)
        decay = jnp.where(slot16 == i, r16[CX * i : CX * (i + 1)], decay)
        part = outside[CX * i : CX * (i + 1)]
        packed_out = jnp.where(slot16 == i, pltpu.roll(part, 2 * KZ * i, 1) if i else part, packed_out)
    v_send[...] = packed_out
    m_send[...] = packed
    m_recv[0] = packed
    m_copies = [
        remote(m_send, m_recv.at[d], m_ss.at[d], m_rs.at[d], {"gx": lax.rem(bx + d, GX)}) for d in range(1, GX)
    ]
    start(m_copies)
    v_copies = [
        remote(v_send, v_recv.at[i], v_ss.at[i], v_rs.at[i], where) for i, where in enumerate((up_x, down_x))
    ]
    start(v_copies)

    end_left, end_right = spread_lanes(left), spread_lanes(pltpu.roll(right, KZ, 1))
    scale = (0.25 / (NC * NC)) * r / (1.0 - r2)
    local = right + left - u
    decay8 = decay * decay
    decay8 = decay8 * decay8
    decay8 = decay8 * decay8
    wrap = 1.0 / (1.0 - decay8)

    w_planes = planes_out(2, w)
    w_rows = [rows_out(2, w, k) for k in range(PARTS)]
    w_edges = [edges_out(2, k) for k in range(PARTS)]

    def fix_of(k):
        edges = z_recv[1, k]

        def step(n, held):
            planes = []
            for j in range(TOGETHER):
                i = TOGETHER * n + j
                x = DEEP * k + i
                a, near = neighbour_sum(res, x + 1, edges, i)
                planes.append([g[x + 1, h, MID, :] + (a[h] + near[h] * INV_DIAG) * INV_DIAG for h in range(2)])
                for h in range(2):
                    w[x + 1, h, MID, :] = planes[j][h]
            return pack_edges(planes, TOGETHER * n, held)

        return step

    for k in ORDER:
        if k in res_planes:
            res_planes[PARTS - 1 - k].wait_recv()
        for copy in res_rows[k] + [res_edges[k]]:
            copy.wait_recv()
        z_send[2, k] = lax.fori_loop(0, DEEP // TOGETHER, fix_of(k), zero)
        if k in w_planes:
            w_planes[k].start()
        start(w_rows[k])
        w_edges[k].start()

    for copy in m_copies + v_copies:
        copy.wait_recv()
    is_right = (iota((CX, 128), 1) // KZ) % 2 == 1
    incoming = jnp.zeros((CX, 128), F32)
    for d in range(GX, 0, -1):
        incoming = jnp.where(is_right, m_recv[d % GX], m_recv[(GX - d) % GX]) + decay * incoming
    incoming = incoming * wrap

    def unpack(a):
        return jnp.concatenate(
            [pltpu.roll(a, 128 - 2 * KZ * i, 1) if i else a for i in range(8)], axis=0
        )

    unpacked = unpack(incoming)
    in_left, in_right = spread_lanes(unpacked), spread_lanes(pltpu.roll(unpacked, 128 - KZ, 1))
    near_out = unpack(jnp.where(is_right, v_recv[0], v_recv[1]))
    near_high, near_low = spread_lanes(near_out), spread_lanes(pltpu.roll(near_out, 128 - KZ, 1))
    solved = scale * (local + from_low * in_right + from_high * in_left)
    turned = r - inverse
    before = scale * (out_low + r * end_left + in_right + r16 * (r * in_left) + turned * near_low)
    after = scale * (out_high + r * end_right + in_left + r16 * (r * in_right) + turned * near_high)

    lines = dot_left(iy, jnp.concatenate([pltpu.roll(solved, KZ * me, 1), before, after], axis=1))
    diagonal = iota((CY, 128), 0) == iota((CY, 128), 1) // KZ
    for b in range(GY):
        rows = slice(ROWS * b, ROWS * b + CY)
        c_send[b] = lines[ROWS * b : ROWS * (b + 1), :128]
        for side in range(2):
            plane = jnp.where(diagonal, lines[rows, 128 * (side + 1) : 128 * (side + 2)], 0.0)
            c_send[b, CY + 2 + side : CY + 3 + side, :] = jnp.sum(plane, axis=0, keepdims=True)

    def copy_c(t, slot):
        return remote(c_send.at[lax.rem(t, GY)], c_recv.at[slot], c_ss.at[t], c_rs.at[slot], of_group(t))

    others(lambda t: copy_c(t, me).start())
    c_recv[me] = c_send[by]

    def before_of(k):
        edges = z_recv[2, k]

        def step(n, carry):
            for j in range(TOGETHER):
                i = TOGETHER * n + j
                x = DEEP * k + i
                a, near = neighbour_sum(w, x + 1, edges, i)
                for h in range(2):
                    rs[x, h] = rs[x, h] - (DIAG * a[h] - near[h])
            return carry

        return step

    for k in ORDER:
        if k in w_planes:
            w_planes[PARTS - 1 - k].wait_recv()
        for copy in w_rows[k] + [w_edges[k]]:
            copy.wait_recv()
        lax.fori_loop(0, DEEP // TOGETHER, before_of(k), 0)

    others(lambda t: copy_c(t, t).wait_recv())

    group = iota((ROWS, 128), 1) // KZ

    def gather(X):
        out = jnp.zeros((ROWS, 128), F32)
        for t in range(GROUP):
            out = jnp.where(group == lax.rem(X + t, CX), c_recv[t], out)
        basis[X + 1] = pltpu.roll(out, lax.rem(128 - KZ * X + 128, 128), 1)

    def gather_step(i, carry):
        gather(2 * i)
        gather(2 * i + 1)
        return carry

    lax.fori_loop(0, CX // 2, gather_step, 0)
    spot = iota((CY, 128), 1) // KZ
    for side, X in ((0, 0), (1, CX + 1)):
        out = jnp.zeros((CY, 128), F32)
        for t in range(GROUP):
            line = jnp.where(diagonal, c_recv[t, CY + 2 + side : CY + 3 + side, :], 0.0)
            for move in (8, 16, 32, 64):
                line = line + pltpu.roll(line, move, 1)
            out = jnp.where(spot == t, line, out)
        basis[X, 0:CY, :] = out
        basis[X, CY:, :] = jnp.zeros((ROWS - CY, 128), F32)

    pz[...] = dot_right(basis[...].reshape((CX + 2) * ROWS, NC), iz).reshape(CX + 2, ROWS, 2 * BZ)

    def put(ref, X, h, four):
        for a in range(4):
            ref[X, h, pl.ds(a, CY, stride=4), :] = four[a]

    for X in (0, CX + 1):
        for h in range(2):
            put(corr, X, h, [pz[X, 0:CY, 128 * h : 128 * (h + 1)]] * 4)

    def prolong(X, carry):
        row = iota((CY, 128), 0)
        for h in range(2):
            lanes = slice(128 * h, 128 * (h + 1))
            here = pz[X, 0:CY, lanes]
            base = pz[X, 0:CY, BZ + 128 * h : BZ + 128 * (h + 1)]
            below = jnp.where(row == 0, pz[X, CY : CY + 1, lanes], pltpu.roll(here, 1, 0))
            above = jnp.where(row == CY - 1, pz[X, CY + 1 : CY + 2, lanes], pltpu.roll(here, CY - 1, 0))
            put(corr, X, h, [here] * 4)
            put(shift, X - 1, h, [base + (here - below), base, base, base + (here - above)])
        return carry

    lax.fori_loop(1, CX + 1, prolong, 0)

    def finish(X, total):
        for h in range(2):
            here = corr[X + 1, h]
            within = shift[X, h]
            low = here - corr[X, h]
            high = here - corr[X + 2, h]
            for j in range(4):
                x = 4 * X + j
                lanes = slice(128 * h, 128 * (h + 1))
                up_ref[x, :, lanes] = w[x + 1, h, MID, :] + here
                out = rs[x, h] - within
                if j == 0:
                    out = out - low
                if j == 3:
                    out = out - high
                new_ref[x, :, lanes] = out
                total = total + (out * out).reshape(8, 8, 128).sum(axis=0)
        return total

    total = lax.fori_loop(0, CX, finish, jnp.zeros((8, 128), F32))

    n_send[...] = total

    def copy_n(t, slot):
        return remote(n_send, n_recv.at[slot], n_ss.at[t], n_rs.at[slot], of_group(t))

    others(lambda t: copy_n(t, me).start())
    n_recv[me] = total
    others(lambda t: copy_n(t, t).wait_recv())
    total = n_recv[0]
    for t in range(1, GROUP):
        total = total + n_recv[t]
    n_held[...] = total

    def copy_l(d):
        to, slot = lax.rem(bx + d, GX), lax.rem(bx + GX - d, GX)
        return (
            remote(n_held, n_last.at[bx], l_ss.at[d], l_rs.at[bx], {"gx": to}),
            remote(n_held, n_last.at[slot], l_ss.at[d], l_rs.at[slot], {"gx": to}),
        )

    line = [copy_l(d) for d in range(1, GX)]
    for out, _ in line:
        out.start()
    n_last[bx] = total
    for _, back in line:
        back.wait_recv()
    total = n_last[0]
    for b in range(1, GX):
        total = total + n_last[b]
    norm_ref[...] = jnp.sqrt(jnp.full((8, 128), jnp.sum(total), F32))

    for copy in list(g_planes.values()) + list(res_planes.values()) + list(w_planes.values()):
        copy.wait_send()
    for copies in g_rows + res_rows + w_rows + [g_edges, res_edges, w_edges, m_copies, v_copies]:
        for copy in copies:
            copy.wait_send()

    def all_sent(t):
        copy_a(t, t).wait_send()
        copy_c(t, t).wait_send()
        copy_n(t, t).wait_send()

    others(all_sent)
    for out, _ in line:
        out.wait_send()


ANY = pl.BlockSpec(memory_space=pl.ANY)
IN_VMEM = pl.BlockSpec(memory_space=pltpu.VMEM)
DMA = pltpu.SemaphoreType.DMA
VMEM = pltpu.VMEM


def per_device(right_side, guess):
    shape = jax.ShapeDtypeStruct
    block = (BX, BY, BZ)
    padded = (BX + 2, 2, PADDED, 128)
    updated, new_residual, norm = pl.pallas_call(
        kernel,
        out_shape=(shape(block, F32), shape(block, F32), shape((8, 128), F32)),
        in_specs=[ANY] * 2,
        out_specs=(IN_VMEM,) * 3,
        scratch_shapes=[
            VMEM(padded, F32), VMEM((BX, 2, BY, 128), F32), VMEM(padded, F32), VMEM(padded, F32),
            VMEM((2, 2 * BZ, NC), BF16), VMEM((2, NC, 2 * BZ), BF16), VMEM((2, NC, GY * ROWS), BF16),
            VMEM((2, GY * ROWS, NC), BF16), VMEM((2, NC, NC), BF16),
            VMEM((4, BY, 128), F32), VMEM((CX, CY, 2 * BZ), F32), VMEM((2, 4 * CX, 128), F32),
            VMEM((CX, ROWS, 128), F32), VMEM((GROUP, ROWS, 128), F32), VMEM((GROUP, ROWS, 128), F32),
            VMEM((CX, 128), F32), VMEM((GX, CX, 128), F32), VMEM((CX, 128), F32), VMEM((2, CX, 128), F32),
            VMEM((GY, ROWS, 128), F32), VMEM((GROUP, ROWS, 128), F32),
            VMEM((3, PARTS, 16, 128), F32), VMEM((3, PARTS, 16, 128), F32),
            VMEM((CX + 2, ROWS, 128), F32), VMEM((CX + 2, ROWS, 2 * BZ), F32),
            VMEM((CX + 2, 2, BY, 128), F32), VMEM((CX, 2, BY, 128), F32),
            VMEM((8, 128), F32), VMEM((GROUP, 8, 128), F32), VMEM((8, 128), F32), VMEM((GX, 8, 128), F32),
            DMA((LOADS, 2)), DMA((LOADS, 2)), DMA((2,)), DMA((2,)),
            DMA((3, 2)), DMA((3, 2)), DMA((3, PARTS, 2)), DMA((3, PARTS, 2)),
            DMA((3, PARTS)), DMA((3, PARTS)), DMA((GROUP,)), DMA((GROUP,)), DMA((GX,)), DMA((GX,)),
            DMA((GROUP,)), DMA((GROUP,)), DMA((GROUP,)), DMA((GROUP,)), DMA((GX,)), DMA((GX,)),
        ],
        compiler_params=pltpu.CompilerParams(
            collective_id=0, has_side_effects=True, vmem_limit_bytes=44 * 1024 * 1024
        ),
        name="schwarz",
    )(right_side, guess)
    return updated, new_residual, norm[0, 0]


def solution(mesh):
    spec = P("gx", "gy", "gz")
    return jax.shard_map(
        per_device, mesh=mesh, in_specs=(spec, spec), out_specs=(spec, spec, P()), check_vma=False
    )
```

time: 71.4 us -> 52.8 us (0.74)
  Pallas kernels: 58.7 us -> 47.5 us
  local copies, waits for them, and re-layouts: 11.6 us -> 4.54 us
    pallas_call x1, Pallas kernels: 58.7 us -> 47.5 us  [per_device(): pl.pallas_call(kernel, out_shape=(shape(block, F32), shape(block, F32), s...]
    unnamed x16 -> x2, local copies, waits for them, and re-layouts: 11.1 us -> 4.03 us
where the time goes in v3:
time: 52.8 us; the launch traced here: 52.7 us
  Pallas kernels  47.5 us (90%)
  local copies, waits for them, and re-layouts  4.54 us (9%)
  between operations  0.64 us (1%)
    pallas_call x1, Pallas kernels, per_device(): pl.pallas_call(kernel, out_shape=(shape(block, F32), shape(block, F32), s...  47.5 us
    unnamed x2, local copies, waits for them, and re-layouts  4.03 us

profile of v3, /device:TPU:1, one launch (start us, length us, event | category | flops | bytes accessed | tf_op | source)
XLA Modules:
  0.0 52.7 jit_solution(12331367496918479206)
XLA Ops:
  0.6 47.5 %schwarz.1 = (f32[64,64,256]{2,1,0:T(8,128)S(1)}, f32[64,64,256]{2,1,0:T(8,128)S(1)}, f32[8,128]{1,0:T(8,128)S(1)}) custom-call(f32[64,64,256]{2,1,0:T(8,128)} %rs_hbm.1, f32[64,64,256]{2,1,0:T(8,128)} %g_hbm.1), custom_call_target="tpu_custom_call" | custom-call | tf_op jit(solution)/shard_map/schwarz/pallas_call | solution.py:696
  48.2 0.5 slice.3
  48.7 2.0 %copy.7 = f32[64,64,256]{2,1,0:T(8,128)} copy(f32[64,64,256]{2,1,0:T(8,128)S(1)} %get-tuple-element.12) | data formatting | bytes 8388608
  50.7 2.0 %copy.8 = f32[64,64,256]{2,1,0:T(8,128)} copy(f32[64,64,256]{2,1,0:T(8,128)S(1)} %get-tuple-element.13) | data formatting | bytes 8388608

commit v4 on v3

--- a/solution.py
+++ b/solution.py
@@ -21,6 +21,7 @@
 GX, GY, GZ = 8, 8, 2
 GROUP = GY * GZ
 KZ = NC // GROUP
+EXTRA = 4
 ROWS = 24
 LOADS = 8
 PLANES = BX // LOADS
@@ -125,10 +126,10 @@
 def kernel(
     rs_hbm, g_hbm,
     up_ref, new_ref, norm_ref,
-    g, rs, res, w, fz, iz, fy, iy, py,
-    fold, folded, extra, spec, a_send, a_recv, m_send, m_recv, v_send, v_recv, c_send, c_recv,
+    g, rs, res, w, fz, iz, py, fe, ie,
+    fold, folded, extra, spec, a_send, a_recv, ae_send, ae_recv, lines_e, m_send, m_recv, v_send, v_recv, c_send, c_recv, ce_send, ce_recv,
     z_send, z_recv, basis, pz, corr, shift, n_send, n_recv, n_held, n_last,
-    g_sem, rs_sem, v_ss, v_rs, x_ss, x_rs, y_ss, y_rs, z_ss, z_rs, a_ss, a_rs, m_ss, m_rs, c_ss, c_rs,
+    g_sem, rs_sem, v_ss, v_rs, x_ss, x_rs, y_ss, y_rs, z_ss, z_rs, a_ss, a_rs, m_ss, m_rs, c_ss, c_rs, ae_ss, ae_rs, ce_ss, ce_rs,
     n_ss, n_rs, l_ss, l_rs,
 ):
     bx, by, bz = lax.axis_index("gx"), lax.axis_index("gy"), lax.axis_index("gz")
@@ -143,11 +144,16 @@
         return pltpu.make_async_remote_copy(src, dst, send, recv, device_id=where, device_id_type=MESH)
 
     def others(body):
-        def step(d, carry):
-            body(lax.rem(me + d, GROUP))
+        def across(d, carry):
+            body((1 - bz) * GY + lax.rem(by + d, GY))
             return carry
 
-        lax.fori_loop(1, GROUP, step, 0)
+        def along(d, carry):
+            body(bz * GY + lax.rem(by + d, GY))
+            return carry
+
+        lax.fori_loop(0, GY, across, 0)
+        lax.fori_loop(1, GY, along, 0)
 
     barrier = pltpu.get_barrier_semaphore()
 
@@ -189,6 +195,14 @@
         for copy in copies:
             copy.wait()
 
+    def wait_recv(copies):
+        for copy in copies:
+            copy.wait_recv()
+
+    def wait_send(copies):
+        for copy in copies:
+            copy.wait_send()
+
     start(load_g[0])
     start(load_g[LOADS - 1])
     start(load_rs[0])
@@ -223,15 +237,13 @@
     keep(py, whole, whole, cas(iota((NC, NC), 0) * iota((NC, NC), 1)))
 
     def place_of(index):
-        b = (index * 2731) >> 16
-        Y = index - ROWS * b
-        place = CY * b + jnp.where(Y == CY, -1, jnp.where(Y == CY + 1, CY, Y))
-        return place, Y < CY + 2
-
-    place, used = place_of(iota((NC, GY * ROWS), 1))
-    keep(fy, whole, whole, jnp.where(used, cas(place * iota((NC, GY * ROWS), 0)), 0.0))
-    place, used = place_of(iota((GY * ROWS, NC), 0))
-    keep(iy, whole, whole, jnp.where(used, cas(place * iota((GY * ROWS, NC), 1)), 0.0))
+        e = index % EXTRA
+        return CY * (index // EXTRA) + jnp.where(e == 0, -1, CY), e < 2
+
+    place, used = place_of(iota((NC, GY * EXTRA), 1))
+    keep(fe, whole, whole, jnp.where(used, cas(place * iota((NC, GY * EXTRA), 0)), 0.0))
+    place, used = place_of(iota((GY * EXTRA, NC), 0))
+    keep(ie, whole, whole, jnp.where(used, cas(place * iota((GY * EXTRA, NC), 1)), 0.0))
 
     wait(load_g[0])
     wait(load_g[LOADS - 1])
@@ -314,64 +326,55 @@
     g_rows = [rows_out(0, g, k) for k in range(PARTS)]
     g_edges = [edges_out(0, k) for k in range(PARTS)]
 
-    def send_part(k):
-        start(g_rows[k])
-        g_edges[k].start()
-
     wait(load_rs[0])
     fold_plane(0, has_below=False)
     for c in range(1, LOADS - 1):
         wait(load_g[c])
         wait(load_rs[c])
         lax.fori_loop(2 * c - 1, 2 * c + 1, fold_step, 0)
-        if c == 4:
-            pl.semaphore_wait(barrier, GX - 1 + GROUP - 1)
-            start(g_planes.values())
-            send_part(0)
-            send_part(1)
-    send_part(2)
     wait(load_rs[LOADS - 1])
     lax.fori_loop(CX - 3, CX - 1, fold_step, 0)
     fold_plane(CX - 1, has_above=False)
-    send_part(3)
-
-    spec[:, 0:CY, :] = dot_right(folded[...].reshape(CX * CY, 2 * BZ), fz).reshape(CX, CY, NC)
+
+    spec[...] = dot_right(folded[...].reshape(CX * CY, 2 * BZ), fz).reshape(CX, CY, NC)
     more = dot_right(jnp.concatenate([extra[0], extra[1]], axis=1), fz.at[:, 0:BZ])
-    for X in range(CX):
-        spec[X, CY : CY + 1, :] = more[X : X + 1]
-        spec[X, CY + 1 : CY + 2, :] = more[CX + X : CX + X + 1]
-        if X:
-            spec[X, 0 : CY + 2, :] = pltpu.roll(spec[X], KZ * X, 1)[0 : CY + 2]
+    for X in range(1, CX):
+        spec[X] = pltpu.roll(spec[X], KZ * X, 1)
     row = iota((CY, 128), 0)
     group = iota((CY, 128), 1) // KZ
     sides = []
-    for side in range(2):
-        plane = more[(2 + side) * CX : (3 + side) * CX]
+    for e in range(EXTRA):
+        plane = more[CX * e : CX * (e + 1)]
         for bit in (1, 2, 4, 8):
             plane = jnp.where((row // bit) % 2 == 1, pltpu.roll(plane, KZ * bit, 1), plane)
         sides.append(plane)
-
-    wide = iota((ROWS, 128), 1) // KZ
-
-    def message_a(t, ref, slot):
-        out = jnp.zeros((ROWS, 128), F32)
+    pl.semaphore_wait(barrier, GX - 1 + GROUP - 1)
+
+    def message_a(t, ref, ref_e, slot):
+        out = jnp.zeros((CY, 128), F32)
         for X in range(CX):
-            out = jnp.where(wide == lax.rem(t + X, CX), spec[X], out)
+            out = jnp.where(group == lax.rem(t + X, CX), spec[X], out)
         ref[slot] = out
-        turn = (row + t) % CX
-        for side in range(2):
-            line = jnp.sum(jnp.where(group == turn, sides[side], 0.0), axis=0, keepdims=True)
-            ref[slot, CY + 2 + side : CY + 3 + side, :] = line
+        turn = group == (row + t) % CX
+        for e in range(EXTRA):
+            ref_e[slot, e : e + 1, :] = jnp.sum(jnp.where(turn, sides[e], 0.0), axis=0, keepdims=True)
 
     def copy_a(t, slot):
-        return remote(a_send.at[t], a_recv.at[slot], a_ss.at[t], a_rs.at[slot], of_group(t))
+        return (
+            remote(a_send.at[t], a_recv.at[slot], a_ss.at[t], a_rs.at[slot], of_group(t)),
+            remote(ae_send.at[t], ae_recv.at[slot], ae_ss.at[t], ae_rs.at[slot], of_group(t)),
+        )
 
     def send_a(t):
-        message_a(t, a_send, t)
-        copy_a(t, me).start()
+        message_a(t, a_send, ae_send, t)
+        start(copy_a(t, me))
 
     others(send_a)
-    message_a(me, a_recv, me)
+    message_a(me, a_recv, ae_recv, me)
+    start(g_planes.values())
+    for k in ORDER:
+        start(g_rows[k])
+        g_edges[k].start()
 
     place = iota((NC, 128), 1) // KZ
     wave = SCREEN * 16.0 + wave_of(iota((NC, 128), 0)) + wave_of(KZ * me + iota((NC, 128), 1) % KZ)
@@ -387,50 +390,19 @@
         from_low = from_low * jnp.where(has, power, 1.0)
         from_high = from_high * jnp.where(has, 1.0, power)
 
-    for copy in g_planes.values():
-        copy.wait_recv()
-    res_planes = planes_out(1, res)
-    res_rows = [rows_out(1, res, k) for k in range(PARTS)]
-    res_edges = [edges_out(1, k) for k in range(PARTS)]
-
-    def residual_of(k):
-        edges = z_recv[0, k]
-
-        def step(n, held):
-            planes = []
-            for j in range(TOGETHER):
-                i = TOGETHER * n + j
-                x = DEEP * k + i
-                a, near = neighbour_sum(g, x + 1, edges, i)
-                planes.append([rs[x, h] - (DIAG * a[h] - near[h]) for h in range(2)])
-                for h in range(2):
-                    res[x + 1, h, MID, :] = planes[j][h]
-            return pack_edges(planes, TOGETHER * n, held)
-
-        return step
-
-    zero = jnp.zeros((16, 128), F32)
-    for k in ORDER:
-        for copy in g_rows[k] + [g_edges[k]]:
-            copy.wait_recv()
-        z_send[1, k] = lax.fori_loop(0, DEEP // TOGETHER, residual_of(k), zero)
-        if k in res_planes:
-            res_planes[k].start()
-        start(res_rows[k])
-        res_edges[k].start()
-
-    others(lambda t: copy_a(t, t).wait_recv())
-    lines = a_recv[0:GY] + a_recv[GY:GROUP]
-    turn = (row + me) % CX
-    beyond = [
-        jnp.concatenate(
-            [jnp.where(group == turn, lines[b, CY + 2 + side : CY + 3 + side], 0.0) for b in range(GY)], axis=0
-        )
-        for side in range(2)
-    ]
-    clean = jnp.where(iota((GY, ROWS, 128), 1) < CY + 2, lines, 0.0).reshape(GY * ROWS, 128)
-    u = pltpu.roll(dot_left(fy, clean), lax.rem(128 - KZ * me + 128, 128), 1)
-    beyond = dot_left(py, jnp.concatenate(beyond, axis=1))
+    others(lambda t: wait_recv(copy_a(t, t)))
+    lines = (a_recv[0:GY] + a_recv[GY:GROUP]).reshape(NC, 128)
+    turn = group == (row + me) % CX
+    beyond = [[], []]
+    for b in range(GY):
+        four = ae_recv[b] + ae_recv[GY + b]
+        lines_e[EXTRA * b : EXTRA * (b + 1), :] = four
+        for side in range(2):
+            beyond[side].append(jnp.where(turn, four[2 + side : 3 + side], 0.0))
+    u = dot_left(py, lines) + dot_left(fe, lines_e[...])
+    u = pltpu.roll(u, lax.rem(128 - KZ * me + 128, 128), 1)
+    beyond = jnp.concatenate([jnp.concatenate(beyond[side], axis=0) for side in range(2)], axis=1)
+    beyond = dot_left(py, beyond)
     out_low, out_high = beyond[:, :128], beyond[:, 128:]
     for move in (8, 16, 32, 64):
         out_low = out_low + pltpu.roll(out_low, move, 1)
@@ -475,6 +447,83 @@
     decay8 = decay8 * decay8
     wrap = 1.0 / (1.0 - decay8)
 
+    for copy in g_planes.values():
+        copy.wait_recv()
+    res_planes = planes_out(1, res)
+    res_rows = [rows_out(1, res, k) for k in range(PARTS)]
+    res_edges = [edges_out(1, k) for k in range(PARTS)]
+
+    def residual_of(k):
+        edges = z_recv[0, k]
+
+        def step(n, held):
+            planes = []
+            for j in range(TOGETHER):
+                i = TOGETHER * n + j
+                x = DEEP * k + i
+                a, near = neighbour_sum(g, x + 1, edges, i)
+                planes.append([rs[x, h] - (DIAG * a[h] - near[h]) for h in range(2)])
+                for h in range(2):
+                    res[x + 1, h, MID, :] = planes[j][h]
+            return pack_edges(planes, TOGETHER * n, held)
+
+        return step
+
+    zero = jnp.zeros((16, 128), F32)
+    for k in ORDER:
+        for copy in g_rows[k] + [g_edges[k]]:
+            copy.wait_recv()
+        z_send[1, k] = lax.fori_loop(0, DEEP // TOGETHER, residual_of(k), zero)
+        if k in res_planes:
+            res_planes[k].start()
+        start(res_rows[k])
+        res_edges[k].start()
+
+    for copy in m_copies + v_copies:
+        copy.wait_recv()
+    is_right = (iota((CX, 128), 1) // KZ) % 2 == 1
+    incoming = jnp.zeros((CX, 128), F32)
+    for d in range(GX, 0, -1):
+        incoming = jnp.where(is_right, m_recv[d % GX], m_recv[(GX - d) % GX]) + decay * incoming
+    incoming = incoming * wrap
+
+    def unpack(a):
+        return jnp.concatenate(
+            [pltpu.roll(a, 128 - 2 * KZ * i, 1) if i else a for i in range(8)], axis=0
+        )
+
+    unpacked = unpack(incoming)
+    in_left, in_right = spread_lanes(unpacked), spread_lanes(pltpu.roll(unpacked, 128 - KZ, 1))
+    near_out = unpack(jnp.where(is_right, v_recv[0], v_recv[1]))
+    near_high, near_low = spread_lanes(near_out), spread_lanes(pltpu.roll(near_out, 128 - KZ, 1))
+    solved = scale * (local + from_low * in_right + from_high * in_left)
+    turned = r - inverse
+    before = scale * (out_low + r * end_left + in_right + r16 * (r * in_left) + turned * near_low)
+    after = scale * (out_high + r * end_right + in_left + r16 * (r * in_right) + turned * near_high)
+
+    back = pltpu.roll(solved, KZ * me, 1)
+    lines = dot_left(py, jnp.concatenate([back, before, after], axis=1))
+    ends = dot_left(ie, back)
+    diagonal = iota((CY, 128), 0) == iota((CY, 128), 1) // KZ
+    for b in range(GY):
+        rows = slice(CY * b, CY * (b + 1))
+        c_send[b] = lines[rows, :128]
+        ce_send[b, 0:2, :] = ends[EXTRA * b : EXTRA * b + 2]
+        for side in range(2):
+            plane = jnp.where(diagonal, lines[rows, 128 * (side + 1) : 128 * (side + 2)], 0.0)
+            ce_send[b, 2 + side : 3 + side, :] = jnp.sum(plane, axis=0, keepdims=True)
+
+    def copy_c(t, slot):
+        b = lax.rem(t, GY)
+        return (
+            remote(c_send.at[b], c_recv.at[slot], c_ss.at[t], c_rs.at[slot], of_group(t)),
+            remote(ce_send.at[b], ce_recv.at[slot], ce_ss.at[t], ce_rs.at[slot], of_group(t)),
+        )
+
+    others(lambda t: start(copy_c(t, me)))
+    c_recv[me] = c_send[by]
+    ce_recv[me] = ce_send[by]
+
     w_planes = planes_out(2, w)
     w_rows = [rows_out(2, w, k) for k in range(PARTS)]
     w_edges = [edges_out(2, k) for k in range(PARTS)]
@@ -506,43 +555,6 @@
         start(w_rows[k])
         w_edges[k].start()
 
-    for copy in m_copies + v_copies:
-        copy.wait_recv()
-    is_right = (iota((CX, 128), 1) // KZ) % 2 == 1
-    incoming = jnp.zeros((CX, 128), F32)
-    for d in range(GX, 0, -1):
-        incoming = jnp.where(is_right, m_recv[d % GX], m_recv[(GX - d) % GX]) + decay * incoming
-    incoming = incoming * wrap
-
-    def unpack(a):
-        return jnp.concatenate(
-            [pltpu.roll(a, 128 - 2 * KZ * i, 1) if i else a for i in range(8)], axis=0
-        )
-
-    unpacked = unpack(incoming)
-    in_left, in_right = spread_lanes(unpacked), spread_lanes(pltpu.roll(unpacked, 128 - KZ, 1))
-    near_out = unpack(jnp.where(is_right, v_recv[0], v_recv[1]))
-    near_high, near_low = spread_lanes(near_out), spread_lanes(pltpu.roll(near_out, 128 - KZ, 1))
-    solved = scale * (local + from_low * in_right + from_high * in_left)
-    turned = r - inverse
-    before = scale * (out_low + r * end_left + in_right + r16 * (r * in_left) + turned * near_low)
-    after = scale * (out_high + r * end_right + in_left + r16 * (r * in_right) + turned * near_high)
-
-    lines = dot_left(iy, jnp.concatenate([pltpu.roll(solved, KZ * me, 1), before, after], axis=1))
-    diagonal = iota((CY, 128), 0) == iota((CY, 128), 1) // KZ
-    for b in range(GY):
-        rows = slice(ROWS * b, ROWS * b + CY)
-        c_send[b] = lines[ROWS * b : ROWS * (b + 1), :128]
-        for side in range(2):
-            plane = jnp.where(diagonal, lines[rows, 128 * (side + 1) : 128 * (side + 2)], 0.0)
-            c_send[b, CY + 2 + side : CY + 3 + side, :] = jnp.sum(plane, axis=0, keepdims=True)
-
-    def copy_c(t, slot):
-        return remote(c_send.at[lax.rem(t, GY)], c_recv.at[slot], c_ss.at[t], c_rs.at[slot], of_group(t))
-
-    others(lambda t: copy_c(t, me).start())
-    c_recv[me] = c_send[by]
-
     def before_of(k):
         edges = z_recv[2, k]
 
@@ -564,15 +576,19 @@
             copy.wait_recv()
         lax.fori_loop(0, DEEP // TOGETHER, before_of(k), 0)
 
-    others(lambda t: copy_c(t, t).wait_recv())
-
-    group = iota((ROWS, 128), 1) // KZ
+    others(lambda t: wait_recv(copy_c(t, t)))
+
+    group_e = iota((EXTRA, 128), 1) // KZ
 
     def gather(X):
-        out = jnp.zeros((ROWS, 128), F32)
+        out, out_e = jnp.zeros((CY, 128), F32), jnp.zeros((EXTRA, 128), F32)
         for t in range(GROUP):
-            out = jnp.where(group == lax.rem(X + t, CX), c_recv[t], out)
-        basis[X + 1] = pltpu.roll(out, lax.rem(128 - KZ * X + 128, 128), 1)
+            place = lax.rem(X + t, CX)
+            out = jnp.where(group == place, c_recv[t], out)
+            out_e = jnp.where(group_e == place, ce_recv[t], out_e)
+        turn = lax.rem(128 - KZ * X + 128, 128)
+        basis[X + 1, 0:CY, :] = pltpu.roll(out, turn, 1)
+        basis[X + 1, CY : CY + EXTRA, :] = pltpu.roll(out_e, turn, 1)
 
     def gather_step(i, carry):
         gather(2 * i)
@@ -584,7 +600,7 @@
     for side, X in ((0, 0), (1, CX + 1)):
         out = jnp.zeros((CY, 128), F32)
         for t in range(GROUP):
-            line = jnp.where(diagonal, c_recv[t, CY + 2 + side : CY + 3 + side, :], 0.0)
+            line = jnp.where(diagonal, ce_recv[t, 2 + side : 3 + side, :], 0.0)
             for move in (8, 16, 32, 64):
                 line = line + pltpu.roll(line, move, 1)
             out = jnp.where(spot == t, line, out)
@@ -636,35 +652,36 @@
 
     total = lax.fori_loop(0, CX, finish, jnp.zeros((8, 128), F32))
 
-    n_send[...] = total
+    one = pl.ds(0, 1)
+    n_send[...] = jnp.broadcast_to(jnp.sum(total, axis=0, keepdims=True), (8, 128))
 
     def copy_n(t, slot):
-        return remote(n_send, n_recv.at[slot], n_ss.at[t], n_rs.at[slot], of_group(t))
+        return remote(n_send.at[one], n_recv.at[slot, one], n_ss.at[t], n_rs.at[slot], of_group(t))
 
     others(lambda t: copy_n(t, me).start())
-    n_recv[me] = total
+    n_recv[me, 0:1, :] = n_send[0:1, :]
     others(lambda t: copy_n(t, t).wait_recv())
-    total = n_recv[0]
+    total = n_recv[0, 0:1, :]
     for t in range(1, GROUP):
-        total = total + n_recv[t]
-    n_held[...] = total
+        total = total + n_recv[t, 0:1, :]
+    n_held[0:1, :] = total
 
     def copy_l(d):
         to, slot = lax.rem(bx + d, GX), lax.rem(bx + GX - d, GX)
         return (
-            remote(n_held, n_last.at[bx], l_ss.at[d], l_rs.at[bx], {"gx": to}),
-            remote(n_held, n_last.at[slot], l_ss.at[d], l_rs.at[slot], {"gx": to}),
+            remote(n_held.at[one], n_last.at[bx, one], l_ss.at[d], l_rs.at[bx], {"gx": to}),
+            remote(n_held.at[one], n_last.at[slot, one], l_ss.at[d], l_rs.at[slot], {"gx": to}),
         )
 
     line = [copy_l(d) for d in range(1, GX)]
     for out, _ in line:
         out.start()
-    n_last[bx] = total
+    n_last[bx, 0:1, :] = total
     for _, back in line:
         back.wait_recv()
-    total = n_last[0]
+    total = n_last[0, 0:1, :]
     for b in range(1, GX):
-        total = total + n_last[b]
+        total = total + n_last[b, 0:1, :]
     norm_ref[...] = jnp.sqrt(jnp.full((8, 128), jnp.sum(total), F32))
 
     for copy in list(g_planes.values()) + list(res_planes.values()) + list(w_planes.values()):
@@ -674,8 +691,8 @@
             copy.wait_send()
 
     def all_sent(t):
-        copy_a(t, t).wait_send()
-        copy_c(t, t).wait_send()
+        wait_send(copy_a(t, t))
+        wait_send(copy_c(t, t))
         copy_n(t, t).wait_send()
 
     others(all_sent)
@@ -700,12 +717,14 @@
         out_specs=(IN_VMEM,) * 3,
         scratch_shapes=[
             VMEM(padded, F32), VMEM((BX, 2, BY, 128), F32), VMEM(padded, F32), VMEM(padded, F32),
-            VMEM((2, 2 * BZ, NC), BF16), VMEM((2, NC, 2 * BZ), BF16), VMEM((2, NC, GY * ROWS), BF16),
-            VMEM((2, GY * ROWS, NC), BF16), VMEM((2, NC, NC), BF16),
+            VMEM((2, 2 * BZ, NC), BF16), VMEM((2, NC, 2 * BZ), BF16), VMEM((2, NC, NC), BF16),
+            VMEM((2, NC, GY * EXTRA), BF16), VMEM((2, GY * EXTRA, NC), BF16),
             VMEM((4, BY, 128), F32), VMEM((CX, CY, 2 * BZ), F32), VMEM((2, 4 * CX, 128), F32),
-            VMEM((CX, ROWS, 128), F32), VMEM((GROUP, ROWS, 128), F32), VMEM((GROUP, ROWS, 128), F32),
+            VMEM((CX, CY, 128), F32), VMEM((GROUP, CY, 128), F32), VMEM((GROUP, CY, 128), F32),
+            VMEM((GROUP, EXTRA, 128), F32), VMEM((GROUP, EXTRA, 128), F32), VMEM((GY * EXTRA, 128), F32),
             VMEM((CX, 128), F32), VMEM((GX, CX, 128), F32), VMEM((CX, 128), F32), VMEM((2, CX, 128), F32),
-            VMEM((GY, ROWS, 128), F32), VMEM((GROUP, ROWS, 128), F32),
+            VMEM((GY, CY, 128), F32), VMEM((GROUP, CY, 128), F32),
+            VMEM((GY, EXTRA, 128), F32), VMEM((GROUP, EXTRA, 128), F32),
             VMEM((3, PARTS, 16, 128), F32), VMEM((3, PARTS, 16, 128), F32),
             VMEM((CX + 2, ROWS, 128), F32), VMEM((CX + 2, ROWS, 2 * BZ), F32),
             VMEM((CX + 2, 2, BY, 128), F32), VMEM((CX, 2, BY, 128), F32),
@@ -713,7 +732,8 @@
             DMA((LOADS, 2)), DMA((LOADS, 2)), DMA((2,)), DMA((2,)),
             DMA((3, 2)), DMA((3, 2)), DMA((3, PARTS, 2)), DMA((3, PARTS, 2)),
             DMA((3, PARTS)), DMA((3, PARTS)), DMA((GROUP,)), DMA((GROUP,)), DMA((GX,)), DMA((GX,)),
-            DMA((GROUP,)), DMA((GROUP,)), DMA((GROUP,)), DMA((GROUP,)), DMA((GX,)), DMA((GX,)),
+            DMA((GROUP,)), DMA((GROUP,)), DMA((GROUP,)), DMA((GROUP,)), DMA((GROUP,)), DMA((GROUP,)),
+            DMA((GROUP,)), DMA((GROUP,)), DMA((GX,)), DMA((GX,)),
         ],
         compiler_params=pltpu.CompilerParams(
             collective_id=0, has_side_effects=True, vmem_limit_bytes=44 * 1024 * 1024

time: 52.8 us -> 54.3 us (1.028)
  Pallas kernels: 47.5 us -> 48.9 us
    pallas_call x1, Pallas kernels: 47.5 us -> 48.9 us  [per_device(): pl.pallas_call(kernel, out_shape=(shape(block, F32), shape(block, F32), s...]
where the time goes in v4:
time: 54.3 us; the launch traced here: 54.1 us
  Pallas kernels  48.9 us (90%)
  local copies, waits for them, and re-layouts  4.54 us (8%)
  between operations  0.64 us (1%)
    pallas_call x1, Pallas kernels, per_device(): pl.pallas_call(kernel, out_shape=(shape(block, F32), shape(block, F32), s...  48.9 us
    unnamed x2, local copies, waits for them, and re-layouts  4.03 us

profile of v4, /device:TPU:1, one launch (start us, length us, event | category | flops | bytes accessed | tf_op | source)
XLA Modules:
  0.0 54.1 jit_solution(2589524780462283545)
XLA Ops:
  0.6 48.9 %schwarz.1 = (f32[64,64,256]{2,1,0:T(8,128)S(1)}, f32[64,64,256]{2,1,0:T(8,128)S(1)}, f32[8,128]{1,0:T(8,128)S(1)}) custom-call(f32[64,64,256]{2,1,0:T(8,128)} %rs_hbm.1, f32[64,64,256]{2,1,0:T(8,128)} %g_hbm.1), custom_call_target="tpu_custom_call" | custom-call | tf_op jit(solution)/shard_map/schwarz/pallas_call | solution.py:713
  49.6 0.5 slice.3
  50.1 2.0 %copy.7 = f32[64,64,256]{2,1,0:T(8,128)} copy(f32[64,64,256]{2,1,0:T(8,128)S(1)} %get-tuple-element.12) | data formatting | bytes 8388608
  52.1 2.0 %copy.8 = f32[64,64,256]{2,1,0:T(8,128)} copy(f32[64,64,256]{2,1,0:T(8,128)S(1)} %get-tuple-element.13) | data formatting | bytes 8388608

commit v5 on v4

--- a/solution.py
+++ b/solution.py
@@ -27,7 +27,7 @@
 PLANES = BX // LOADS
 PARTS = 4
 DEEP = BX // PARTS
-TOGETHER = 4
+TOGETHER = 8
 ORDER = (0, 3, 1, 2)
 TOP = 8
 PADDED = BY + 16
@@ -332,9 +332,19 @@
         wait(load_g[c])
         wait(load_rs[c])
         lax.fori_loop(2 * c - 1, 2 * c + 1, fold_step, 0)
+        if c == 4:
+            pl.semaphore_wait(barrier, GX - 1 + GROUP - 1)
+            start(g_planes.values())
+            for k in (0, 1):
+                start(g_rows[k])
+                g_edges[k].start()
+    start(g_rows[2])
+    g_edges[2].start()
     wait(load_rs[LOADS - 1])
     lax.fori_loop(CX - 3, CX - 1, fold_step, 0)
     fold_plane(CX - 1, has_above=False)
+    start(g_rows[3])
+    g_edges[3].start()
 
     spec[...] = dot_right(folded[...].reshape(CX * CY, 2 * BZ), fz).reshape(CX, CY, NC)
     more = dot_right(jnp.concatenate([extra[0], extra[1]], axis=1), fz.at[:, 0:BZ])
@@ -348,7 +358,6 @@
         for bit in (1, 2, 4, 8):
             plane = jnp.where((row // bit) % 2 == 1, pltpu.roll(plane, KZ * bit, 1), plane)
         sides.append(plane)
-    pl.semaphore_wait(barrier, GX - 1 + GROUP - 1)
 
     def message_a(t, ref, ref_e, slot):
         out = jnp.zeros((CY, 128), F32)
@@ -371,11 +380,6 @@
 
     others(send_a)
     message_a(me, a_recv, ae_recv, me)
-    start(g_planes.values())
-    for k in ORDER:
-        start(g_rows[k])
-        g_edges[k].start()
-
     place = iota((NC, 128), 1) // KZ
     wave = SCREEN * 16.0 + wave_of(iota((NC, 128), 0)) + wave_of(KZ * me + iota((NC, 128), 1) % KZ)
     r = 1.0 / (1.0 + 0.5 * wave + jnp.sqrt(wave + 0.25 * wave * wave))
@@ -389,6 +393,38 @@
         has = (place // bit) % 2 == 1
         from_low = from_low * jnp.where(has, power, 1.0)
         from_high = from_high * jnp.where(has, 1.0, power)
+
+    res_planes = planes_out(1, res)
+    res_rows = [rows_out(1, res, k) for k in range(PARTS)]
+    res_edges = [edges_out(1, k) for k in range(PARTS)]
+
+    def residual_of(k):
+        edges = z_recv[0, k]
+
+        def step(n, held):
+            planes = []
+            for j in range(TOGETHER):
+                i = TOGETHER * n + j
+                x = DEEP * k + i
+                a, near = neighbour_sum(g, x + 1, edges, i)
+                planes.append([rs[x, h] - (DIAG * a[h] - near[h]) for h in range(2)])
+                for h in range(2):
+                    res[x + 1, h, MID, :] = planes[j][h]
+            return pack_edges(planes, TOGETHER * n, held)
+
+        return step
+
+    zero = jnp.zeros((16, 128), F32)
+    for k in ORDER:
+        if k in g_planes:
+            g_planes[PARTS - 1 - k].wait_recv()
+        for copy in g_rows[k] + [g_edges[k]]:
+            copy.wait_recv()
+        z_send[1, k] = lax.fori_loop(0, DEEP // TOGETHER, residual_of(k), zero)
+        if k in res_planes:
+            res_planes[k].start()
+        start(res_rows[k])
+        res_edges[k].start()
 
     others(lambda t: wait_recv(copy_a(t, t)))
     lines = (a_recv[0:GY] + a_recv[GY:GROUP]).reshape(NC, 128)
@@ -447,37 +483,39 @@
     decay8 = decay8 * decay8
     wrap = 1.0 / (1.0 - decay8)
 
-    for copy in g_planes.values():
-        copy.wait_recv()
-    res_planes = planes_out(1, res)
-    res_rows = [rows_out(1, res, k) for k in range(PARTS)]
-    res_edges = [edges_out(1, k) for k in range(PARTS)]
-
-    def residual_of(k):
-        edges = z_recv[0, k]
+    w_planes = planes_out(2, w)
+    w_rows = [rows_out(2, w, k) for k in range(PARTS)]
+    w_edges = [edges_out(2, k) for k in range(PARTS)]
+
+    def fix_of(k):
+        edges = z_recv[1, k]
 
         def step(n, held):
             planes = []
             for j in range(TOGETHER):
                 i = TOGETHER * n + j
                 x = DEEP * k + i
-                a, near = neighbour_sum(g, x + 1, edges, i)
-                planes.append([rs[x, h] - (DIAG * a[h] - near[h]) for h in range(2)])
+                a, near = neighbour_sum(res, x + 1, edges, i)
+                planes.append([g[x + 1, h, MID, :] + (a[h] + near[h] * INV_DIAG) * INV_DIAG for h in range(2)])
                 for h in range(2):
-                    res[x + 1, h, MID, :] = planes[j][h]
+                    w[x + 1, h, MID, :] = planes[j][h]
             return pack_edges(planes, TOGETHER * n, held)
 
         return step
 
-    zero = jnp.zeros((16, 128), F32)
-    for k in ORDER:
-        for copy in g_rows[k] + [g_edges[k]]:
-            copy.wait_recv()
-        z_send[1, k] = lax.fori_loop(0, DEEP // TOGETHER, residual_of(k), zero)
-        if k in res_planes:
-            res_planes[k].start()
-        start(res_rows[k])
-        res_edges[k].start()
+    def fix(parts):
+        for k in parts:
+            if k in res_planes:
+                res_planes[PARTS - 1 - k].wait_recv()
+            for copy in res_rows[k] + [res_edges[k]]:
+                copy.wait_recv()
+            z_send[2, k] = lax.fori_loop(0, DEEP // TOGETHER, fix_of(k), zero)
+            if k in w_planes:
+                w_planes[k].start()
+            start(w_rows[k])
+            w_edges[k].start()
+
+    fix(ORDER)
 
     for copy in m_copies + v_copies:
         copy.wait_recv()
@@ -524,36 +562,6 @@
     c_recv[me] = c_send[by]
     ce_recv[me] = ce_send[by]
 
-    w_planes = planes_out(2, w)
-    w_rows = [rows_out(2, w, k) for k in range(PARTS)]
-    w_edges = [edges_out(2, k) for k in range(PARTS)]
-
-    def fix_of(k):
-        edges = z_recv[1, k]
-
-        def step(n, held):
-            planes = []
-            for j in range(TOGETHER):
-                i = TOGETHER * n + j
-                x = DEEP * k + i
-                a, near = neighbour_sum(res, x + 1, edges, i)
-                planes.append([g[x + 1, h, MID, :] + (a[h] + near[h] * INV_DIAG) * INV_DIAG for h in range(2)])
-                for h in range(2):
-                    w[x + 1, h, MID, :] = planes[j][h]
-            return pack_edges(planes, TOGETHER * n, held)
-
-        return step
-
-    for k in ORDER:
-        if k in res_planes:
-            res_planes[PARTS - 1 - k].wait_recv()
-        for copy in res_rows[k] + [res_edges[k]]:
-            copy.wait_recv()
-        z_send[2, k] = lax.fori_loop(0, DEEP // TOGETHER, fix_of(k), zero)
-        if k in w_planes:
-            w_planes[k].start()
-        start(w_rows[k])
-        w_edges[k].start()
 
     def before_of(k):
         edges = z_recv[2, k]
@@ -591,11 +599,11 @@
         basis[X + 1, CY : CY + EXTRA, :] = pltpu.roll(out_e, turn, 1)
 
     def gather_step(i, carry):
-        gather(2 * i)
-        gather(2 * i + 1)
+        for j in range(4):
+            gather(4 * i + j)
         return carry
 
-    lax.fori_loop(0, CX // 2, gather_step, 0)
+    lax.fori_loop(0, CX // 4, gather_step, 0)
     spot = iota((CY, 128), 1) // KZ
     for side, X in ((0, 0), (1, CX + 1)):
         out = jnp.zeros((CY, 128), F32)
@@ -629,7 +637,10 @@
             put(shift, X - 1, h, [base + (here - below), base, base, base + (here - above)])
         return carry
 
-    lax.fori_loop(1, CX + 1, prolong, 0)
+    def by_two(body):
+        return lambda i, carry: body(2 * i + 1, body(2 * i, carry))
+
+    lax.fori_loop(0, CX // 2, by_two(lambda X, carry: prolong(X + 1, carry)), 0)
 
     def finish(X, total):
         for h in range(2):
@@ -650,7 +661,7 @@
                 total = total + (out * out).reshape(8, 8, 128).sum(axis=0)
         return total
 
-    total = lax.fori_loop(0, CX, finish, jnp.zeros((8, 128), F32))
+    total = lax.fori_loop(0, CX // 2, by_two(finish), jnp.zeros((8, 128), F32))
 
     one = pl.ds(0, 1)
     n_send[...] = jnp.broadcast_to(jnp.sum(total, axis=0, keepdims=True), (8, 128))
@@ -698,6 +709,20 @@
     others(all_sent)
     for out, _ in line:
         out.wait_send()
+
+
+def hand_on(up, new, norm, up_hbm, new_hbm, norm_out, sems):
+    part = BX // 2
+    copies = [
+        pltpu.make_async_copy(src.at[pl.ds(part * k, part)], dst.at[pl.ds(part * k, part)], sems.at[i, k])
+        for k in range(2)
+        for i, (src, dst) in enumerate(((up, up_hbm), (new, new_hbm)))
+    ]
+    for copy in copies:
+        copy.start()
+    norm_out[0, 0] = norm[0, 0]
+    for copy in copies:
+        copy.wait()
 
 
 ANY = pl.BlockSpec(memory_space=pl.ANY)
@@ -740,7 +765,16 @@
         ),
         name="schwarz",
     )(right_side, guess)
-    return updated, new_residual, norm[0, 0]
+    updated, new_residual, norm = pl.pallas_call(
+        hand_on,
+        out_shape=(shape(block, F32), shape(block, F32), shape((1, 1), F32)),
+        in_specs=[ANY, ANY, IN_VMEM],
+        out_specs=(ANY, ANY, pl.BlockSpec(memory_space=pltpu.SMEM)),
+        scratch_shapes=[DMA((2, 2))],
+        compiler_params=pltpu.CompilerParams(vmem_limit_bytes=1024 * 1024),
+        name="hand_on",
+    )(updated, new_residual, norm)
+    return updated, new_residual, norm.reshape(())
 
 
 def solution(mesh):

time: 54.3 us -> 50.2 us (0.924)
  local copies, waits for them, and re-layouts: 4.54 us -> 0 us
    unnamed x2 -> x0, local copies, waits for them, and re-layouts: 4.03 us -> none
    pallas_call x0 -> x1, Pallas kernels: none -> 3.88 us  [per_device(): pl.pallas_call(hand_on, out_shape=(shape(block, F32), shape(block, F32),...]
    pallas_call x1, Pallas kernels: 48.9 us -> 45.4 us  [per_device(): pl.pallas_call(kernel, out_shape=(shape(block, F32), shape(block, F32), s...]
where the time goes in v5:
time: 50.2 us; the launch traced here: 49.9 us
  Pallas kernels  49.3 us (98%)
  between operations  0.64 us (1%)
    pallas_call x1, Pallas kernels, per_device(): pl.pallas_call(kernel, out_shape=(shape(block, F32), shape(block, F32), s...  45.4 us
    pallas_call x1, Pallas kernels, per_device(): pl.pallas_call(hand_on, out_shape=(shape(block, F32), shape(block, F32),...  3.88 us

profile of v5, /device:TPU:1, one launch (start us, length us, event | category | flops | bytes accessed | tf_op | source)
XLA Modules:
  0.0 49.9 jit_solution(12657826853982460869)
XLA Ops:
  0.6 45.4 %schwarz.1 = (f32[64,64,256]{2,1,0:T(8,128)S(1)}, f32[64,64,256]{2,1,0:T(8,128)S(1)}, f32[8,128]{1,0:T(8,128)S(1)}) custom-call(f32[64,64,256]{2,1,0:T(8,128)} %rs_hbm.1, f32[64,64,256]{2,1,0:T(8,128)} %g_hbm.1), custom_call_target="tpu_custom_call" | custom-call | tf_op jit(solution)/shard_map/schwarz/pallas_call | solution.py:738
  46.0 3.9 %hand_on.1 = (f32[64,64,256]{2,1,0:T(8,128)}, f32[64,64,256]{2,1,0:T(8,128)}, f32[1,1]{1,0:T(1,128)}) custom-call(f32[64,64,256]{2,1,0:T(8,128)S(1)} %get-tuple-element.9.up, f32[64,64,256]{2,1,0:T(8,128)S(1)} %get-tuple-element.10.new, f32[8,128]{1,0:T(8,128)S(1)} %get-tuple-element.11.norm), custom_call_target="tpu_custom_call" | custom-call | tf_op jit(solution)/shard_map/hand_on/pallas_call | solution.py:768

commit v6 on v5

--- a/solution.py
+++ b/solution.py
@@ -642,26 +642,31 @@
 
     lax.fori_loop(0, CX // 2, by_two(lambda X, carry: prolong(X + 1, carry)), 0)
 
-    def finish(X, total):
+    def final_residual(X, h):
+        here = corr[X + 1, h]
+        within = shift[X, h]
+        planes = [rs[4 * X + j, h] - within for j in range(4)]
+        planes[0] = planes[0] - (here - corr[X, h])
+        planes[3] = planes[3] - (here - corr[X + 2, h])
+        return here, planes
+
+    def add_squares(X, total):
         for h in range(2):
-            here = corr[X + 1, h]
-            within = shift[X, h]
-            low = here - corr[X, h]
-            high = here - corr[X + 2, h]
-            for j in range(4):
-                x = 4 * X + j
-                lanes = slice(128 * h, 128 * (h + 1))
-                up_ref[x, :, lanes] = w[x + 1, h, MID, :] + here
-                out = rs[x, h] - within
-                if j == 0:
-                    out = out - low
-                if j == 3:
-                    out = out - high
-                new_ref[x, :, lanes] = out
+            _, planes = final_residual(X, h)
+            for out in planes:
                 total = total + (out * out).reshape(8, 8, 128).sum(axis=0)
         return total
 
-    total = lax.fori_loop(0, CX // 2, by_two(finish), jnp.zeros((8, 128), F32))
+    def finish(X, carry):
+        for h in range(2):
+            here, planes = final_residual(X, h)
+            lanes = slice(128 * h, 128 * (h + 1))
+            for j in range(4):
+                up_ref[4 * X + j, :, lanes] = w[4 * X + j + 1, h, MID, :] + here
+                new_ref[4 * X + j, :, lanes] = planes[j]
+        return carry
+
+    total = lax.fori_loop(0, CX // 2, by_two(add_squares), jnp.zeros((8, 128), F32))
 
     one = pl.ds(0, 1)
     n_send[...] = jnp.broadcast_to(jnp.sum(total, axis=0, keepdims=True), (8, 128))
@@ -670,6 +675,7 @@
         return remote(n_send.at[one], n_recv.at[slot, one], n_ss.at[t], n_rs.at[slot], of_group(t))
 
     others(lambda t: copy_n(t, me).start())
+    lax.fori_loop(0, CX // 2, by_two(finish), 0)
     n_recv[me, 0:1, :] = n_send[0:1, :]
     others(lambda t: copy_n(t, t).wait_recv())
     total = n_recv[0, 0:1, :]

time: 50.2 us -> 49.9 us (level)
  no operation moved by 1% of the time
where the time goes in v6:
time: 49.9 us; the launch traced here: 49.7 us
  Pallas kernels  49 us (98%)
  between operations  0.64 us (1%)
    pallas_call x1, Pallas kernels, per_device(): pl.pallas_call(kernel, out_shape=(shape(block, F32), shape(block, F32), s...  45.2 us
    pallas_call x1, Pallas kernels, per_device(): pl.pallas_call(hand_on, out_shape=(shape(block, F32), shape(block, F32),...  3.88 us

profile of v6, /device:TPU:1, one launch (start us, length us, event | category | flops | bytes accessed | tf_op | source)
XLA Modules:
  0.0 49.7 jit_solution(16905417203796403645)
XLA Ops:
  0.6 45.2 %schwarz.1 = (f32[64,64,256]{2,1,0:T(8,128)S(1)}, f32[64,64,256]{2,1,0:T(8,128)S(1)}, f32[8,128]{1,0:T(8,128)S(1)}) custom-call(f32[64,64,256]{2,1,0:T(8,128)} %rs_hbm.1, f32[64,64,256]{2,1,0:T(8,128)} %g_hbm.1), custom_call_target="tpu_custom_call" | custom-call | tf_op jit(solution)/shard_map/schwarz/pallas_call | solution.py:744
  45.8 3.9 %hand_on.1 = (f32[64,64,256]{2,1,0:T(8,128)}, f32[64,64,256]{2,1,0:T(8,128)}, f32[1,1]{1,0:T(1,128)}) custom-call(f32[64,64,256]{2,1,0:T(8,128)S(1)} %get-tuple-element.9.up, f32[64,64,256]{2,1,0:T(8,128)S(1)} %get-tuple-element.10.new, f32[8,128]{1,0:T(8,128)S(1)} %get-tuple-element.11.norm), custom_call_target="tpu_custom_call" | custom-call | tf_op jit(solution)/shard_map/hand_on/pallas_call | solution.py:774
